TPU v7x, 512 devices: a whole 4x8x8 slice. The times are simulated.
512 devices in a mesh: win: 128 (over z, y, core), tile: 4 (over x).
Axes of the slice: x: 4, y: 8, z: 8, core: 2. Of those that a mesh axis runs over, the one named last changes fastest.
Arguments:
- right_side: float32 [128, 2, 128, 1024], P('win', None, 'tile'), may hold values from -64 to 64
- error_weight: float32 [128, 2, 128, 1024], P('win', None, 'tile'), may hold values from 0.5 to 4
- coeffs: float32 [4, 128, 2, 128, 1024], P(None, 'win', None, 'tile'), may hold values from 0.1 to 0.4
- obs_block: int32 [128, 128], P('win', 'tile'), may hold values from 0 to 511
- obs_pos: int32 [128, 128, 128], P('win', 'tile'), may hold values from 0 to 127
- obs_weight: float32 [128, 128, 128], P('win', 'tile'), may hold values from 0.5 to 4
Outputs:
- solution_field: float32 [128, 2, 128, 1024], P('win', None, 'tile')
- residual: float32 [128, 2, 128, 1024], P('win', None, 'tile')
All inputs are finite; a program needn't handle non-finite values.
Results may differ from a plain program's by a relative error of at most 0.0001.
Values sent between devices are 32-bit elements; how exact they have to be, the bound alone decides.
A program may use at most 64 MiB of HBM per device.

v0:
```python
import jax
import jax.numpy as jnp
from jax import lax
from jax.sharding import Mesh
from jax.sharding import PartitionSpec as P

ITERS = 3
WIN = ("win_0", "win_1", "win_2")


def extended(block, sides, width):
    for axis, dim in sides:
        count = lax.axis_size(axis)
        forward = [(i, i + 1) for i in range(count - 1)]
        backward = [(target, source) for source, target in forward]
        low = lax.ppermute(
            lax.slice_in_dim(block, block.shape[dim] - width, None, axis=dim), axis, forward
        )
        high = lax.ppermute(lax.slice_in_dim(block, 0, width, axis=dim), axis, backward)
        block = jnp.concatenate([low, block, high], axis=dim)
    return block


def passed_along(x, axis, by):
    devices = lax.axis_size(axis)
    pairs = [(i, i + by) for i in range(devices) if 0 <= i + by < devices]
    return lax.ppermute(x, axis, pairs)


def sent_to_all(x, axis):
    devices = lax.axis_size(axis)
    return lax.all_to_all(jnp.broadcast_to(x[None], (devices, *x.shape)), axis, 0, 0, tiled=True)


def over_copies(x, axis):
    everything = sent_to_all(x, axis)
    return jnp.sum(everything, axis=0)


def by_axis(x, axes):
    far, near = axes
    nearer = over_copies(x, near)
    return over_copies(nearer, far)


def in_one(arrays, axis):
    ravelled, at, gathered = (jnp.concatenate([a.reshape(-1) for a in arrays]), 0, [])
    running = by_axis(ravelled, axis)
    for a in arrays:
        gathered.append(running[at : at + a.size].reshape(a.shape))
        at += a.size
    return tuple(gathered)


def forward(state, coeffs):
    padded = extended(state, (("tile", 2),), 1)
    north_south = padded[:, :, 2:, :] + padded[:, :, :-2, :]
    return (
        coeffs[0] * state
        + coeffs[1] * north_south
        + coeffs[2] * jnp.roll(state, -1, axis=3)
        + coeffs[3] * jnp.roll(state, 1, axis=3)
    )


def backward(state, coeffs):
    spread = extended(coeffs[1] * state, (("tile", 2),), 1)
    north_south = spread[:, :, 2:, :] + spread[:, :, :-2, :]
    return (
        coeffs[0] * state
        + north_south
        + jnp.roll(coeffs[2] * state, 1, axis=3)
        + jnp.roll(coeffs[3] * state, -1, axis=3)
    )


def observe(state, block_hot, cell_hot, obs_weight):
    width = cell_hot.shape[2]
    block_rows = state.reshape(-1, width)
    picked = jnp.dot(
        block_hot, block_rows, precision=lax.Precision.HIGHEST, preferred_element_type=jnp.float32
    )
    observed = jnp.einsum("bjc,bc->bj", cell_hot, picked, precision=lax.Precision.HIGHEST)
    weighted = observed * obs_weight[0]
    returned = jnp.einsum("bjc,bj->bc", cell_hot, weighted, precision=lax.Precision.HIGHEST)
    spread = jnp.dot(
        block_hot.T, returned, precision=lax.Precision.HIGHEST, preferred_element_type=jnp.float32
    )
    return spread.reshape(state.shape)


def on_device(right_side, error_weight, coeffs, obs_block, obs_pos, obs_weight):
    width = obs_pos.shape[2]
    block_total = right_side.size // width
    block_hot = (obs_block[0][:, None] == jnp.arange(block_total, dtype=jnp.int32)[None, :]).astype(
        jnp.float32
    )
    cell_hot = (obs_pos[0][:, :, None] == jnp.arange(width, dtype=jnp.int32)[None, None, :]).astype(
        jnp.float32
    )
    weight_next = passed_along(error_weight, WIN, -1)

    def hessian(state):
        propagated = forward(state, coeffs)
        before = passed_along(propagated, WIN, 1)
        weighted = error_weight * (state - before)
        later = passed_along(state, WIN, -1)
        following = weight_next * (later - propagated)
        return (
            weighted - backward(following, coeffs) + observe(state, block_hot, cell_hot, obs_weight)
        )

    def two_products(vector, image_vec):
        return in_one(
            (jnp.sum(vector * vector), jnp.sum(vector * image_vec)),
            (("win_0", "win_1"), ("win_2", "tile")),
        )

    solution_field = jnp.zeros_like(right_side)
    residual = right_side
    product_vec = hessian(residual)
    norm_now, product = two_products(residual, product_vec)
    step_length = norm_now / product
    direction = residual
    along = product_vec
    for iteration in range(ITERS):
        solution_field = solution_field + step_length * direction
        residual = residual - step_length * along
        if iteration + 1 < ITERS:
            product_vec = hessian(residual)
            norm_next, product = two_products(residual, product_vec)
            beta_ratio = norm_next / norm_now
            step_length = norm_next / (product - beta_ratio * norm_next / step_length)
            direction = residual + beta_ratio * direction
            along = product_vec + beta_ratio * along
            norm_now = norm_next
    return (solution_field, residual)


def solution(mesh):
    split = Mesh(
        mesh.devices.reshape(8, 8, 2, mesh.shape["tile"]), ("win_0", "win_1", "win_2", "tile")
    )
    in_specs = (
        P(WIN, None, "tile", None),
        P(WIN, None, "tile", None),
        P(None, WIN, None, "tile", None),
        P(WIN, "tile"),
        P(WIN, "tile", None),
        P(WIN, "tile", None),
    )
    out_specs = (P(WIN, None, "tile", None), P(WIN, None, "tile", None))
    return jax.shard_map(
        on_device, mesh=split, in_specs=in_specs, out_specs=out_specs, check_vma=False
    )
```

profile of v0, /device:TPU:1, one launch (start us, length us, event | category | flops | bytes accessed | tf_op | source)
XLA Modules:
  0.0 190.0 jit_solution(7076373985294307808)
XLA Ops:
  0.7 8.9 %collective-permute-start.3 = (f32[1,2,32,1024]{3,2,1,0:T(8,128)}, f32[1,2,32,1024]{3,2,1,0:T(8,128)S(1)}, u32[]{:S(2)}, u32[]{:S(2)}) collective-permute-start(f32[1,2,32,1024]{3,2,1,0:T(8,128)} %param.7), channel_id=1, source_target_pairs={{4,0},{8,4},{12,8},{16,12},{20,16},{24,20},{28,24},{32,28},{36,32}... | collective-permute-start | bytes 786440 | tf_op jit(solution)/shard_map/ppermute | solution.py:27
  9.6 1.9 %collective-permute-start.4 = (f32[1,2,32,1024]{3,2,1,0:T(8,128)}, f32[1,2,32,1024]{3,2,1,0:T(8,128)S(1)}, u32[]{:S(2)}, u32[]{:S(2)}) collective-permute-start(f32[1,2,32,1024]{3,2,1,0:T(8,128)} %param.6), channel_id=1, source_target_pairs={{4,0},{8,4},{12,8},{16,12},{20,16},{24,20},{28,24},{32,28},{36,32}... | collective-permute-start | bytes 786440 | tf_op jit(solution)/shard_map/ppermute | solution.py:27
  11.5 0.9 fusion.72
  12.4 1.3 collective-permute-start
  13.7 4.0 %collective-permute-start.1 = (f32[1,2,1,1024]{3,2,1,0:T(1,128)S(1)}, f32[1,2,1,1024]{3,2,1,0:T(1,128)S(1)}, u32[]{:S(2)}, u32[]{:S(2)}) collective-permute-start(f32[1,2,1,1024]{3,2,1,0:T(1,128)S(1)} %get-tuple-element.47), channel_id=1, source_target_pairs={{0,1},{1,2},{2,3},{4,5},{5,6},{6,7},{8,9},{9,10},{10,11},{12,13},{... | collective-permute-start | bytes 24584 | tf_op jit(solution)/shard_map/ppermute | solution.py:16
  17.7 1.0 reshape.313
  18.7 1.2 fusion.73
  19.9 0.2 fusion.50
  20.2 2.0 %fusion.5 = f32[32,1,128]{2,1,0:T(1,128)S(1)} fusion(f32[32,128,1]{1,2,0:T(1,128)S(1)} %bitcast.136, s32[32,128]{1,0:T(8,128)S(1)} %bitcast.145), kind=kOutput, calls=%fused_computation.6 | convolution fusion | flops 6815744 | bytes 49152 | tf_op jit(solution)/shard_map/bjc,bc->bj/dot_general | solution.py:83
  22.2 1.5 fusion.4
  23.7 0.9 bitcast_multiply_fusion.2
  24.7 4.3 %collective-permute-start.2 = (f32[1,2,32,1024]{3,2,1,0:T(8,128)}, f32[1,2,32,1024]{3,2,1,0:T(8,128)}, u32[]{:S(2)}, u32[]{:S(2)}) collective-permute-start(f32[1,2,32,1024]{3,2,1,0:T(8,128)} %get-tuple-element.19), channel_id=1, source_target_pairs={{0,4},{4,8},{8,12},{12,16},{16,20},{20,24},{24,28},{28,32},{32,36}... | collective-permute-start | bytes 786440 | tf_op jit(solution)/shard_map/ppermute | solution.py:27
  29.1 1.3 collective-permute-start.5
  30.4 4.0 %collective-permute-start.6 = (f32[1,2,1,1024]{3,2,1,0:T(1,128)S(1)}, f32[1,2,1,1024]{3,2,1,0:T(1,128)S(1)}, u32[]{:S(2)}, u32[]{:S(2)}) collective-permute-start(f32[1,2,1,1024]{3,2,1,0:T(1,128)S(1)} %get-tuple-element.45), channel_id=1, source_target_pairs={{0,1},{1,2},{2,3},{4,5},{5,6},{6,7},{8,9},{9,10},{10,11},{12,13},{... | collective-permute-start | bytes 24584 | tf_op jit(solution)/shard_map/ppermute | solution.py:16
  34.4 0.5 fusion.49
  34.9 0.1 slice.272
  35.2 1.8 multiply_reduce_fusion.5
  37.0 1.4 pad_maximum_fusion.12
  38.3 8.3 %all_to_all.36 = f32[8,1,2]{2,1,0:T(1,128)S(1)} all-to-all(f32[8,1,2]{2,1,0:T(1,128)S(1)} %broadcast_in_dim.12), channel_id=1, replica_groups=mesh['win_0'=8,'win_1'=8,'win_2'=2,'tile'=4] {'win_2','tile'}, dimensions={0} | all-to-all | bytes 128 | tf_op jit(solution)/shard_map/all_to_all | solution.py:32
  46.7 22.9 %all_to_all.37 = f32[64,1,2]{2,1,0:T(1,128)S(1)} all-to-all(f32[64,1,2]{2,1,0:T(1,128)S(1)} %broadcast_in_dim.13), channel_id=1, replica_groups=mesh['win_0'=8,'win_1'=8,'win_2'=2,'tile'=4] {'win_0','win_1'}, dimensions={0} | all-to-all | bytes 1024 | tf_op jit(solution)/shard_map/all_to_all | solution.py:32
  69.6 0.1 reduce_sum.111
  69.7 0.6 fusion.77
  71.6 0.1 fusion.69
  71.8 4.0 %collective-permute-start.10 = (f32[1,2,32,1024]{3,2,1,0:T(8,128)S(1)}, f32[1,2,32,1024]{3,2,1,0:T(8,128)S(1)}, u32[]{:S(2)}, u32[]{:S(2)}) collective-permute-start(f32[1,2,32,1024]{3,2,1,0:T(8,128)S(1)} %multiply_subtract_fusion.2), channel_id=1, source_target_pairs={{4,0},{8,4},{12,8},{16,12},{20,16},{24,20},{28,24},{32,28},{36,32}... | collective-permute-start | bytes 786440 | tf_op jit(solution)/shard_map/ppermute | solution.py:27
  75.9 1.3 collective-permute-start.7
  77.2 4.0 %collective-permute-start.8 = (f32[1,2,1,1024]{3,2,1,0:T(1,128)S(1)}, f32[1,2,1,1024]{3,2,1,0:T(1,128)S(1)}, u32[]{:S(2)}, u32[]{:S(2)}) collective-permute-start(f32[1,2,1,1024]{3,2,1,0:T(1,128)S(1)} %get-tuple-element.39), channel_id=1, source_target_pairs={{0,1},{1,2},{2,3},{4,5},{5,6},{6,7},{8,9},{9,10},{10,11},{12,13},{... | collective-permute-start | bytes 24584 | tf_op jit(solution)/shard_map/ppermute | solution.py:16
  81.2 0.2 fusion.48
  81.5 2.0 %fusion.3 = f32[32,1,128]{2,1,0:T(1,128)S(1)} fusion(f32[32,128,1]{1,2,0:T(1,128)S(1)} %bitcast.139, s32[32,128]{1,0:T(8,128)S(1)} %bitcast.147), kind=kOutput, calls=%fused_computation.4 | convolution fusion | flops 6815744 | bytes 49152 | tf_op jit(solution)/shard_map/bjc,bc->bj/dot_general | solution.py:83
  83.5 1.5 fusion.2
  85.0 0.7 copy-done.7
  85.7 1.9 bitcast_multiply_fusion.1
  87.6 2.7 %collective-permute-start.9 = (f32[1,2,32,1024]{3,2,1,0:T(8,128)}, f32[1,2,32,1024]{3,2,1,0:T(8,128)}, u32[]{:S(2)}, u32[]{:S(2)}) collective-permute-start(f32[1,2,32,1024]{3,2,1,0:T(8,128)} %get-tuple-element.15), channel_id=1, source_target_pairs={{0,4},{4,8},{8,12},{12,16},{16,20},{20,24},{24,28},{28,32},{32,36}... | collective-permute-start | bytes 786440 | tf_op jit(solution)/shard_map/ppermute | solution.py:27
  90.3 1.3 collective-permute-start.11
  91.6 4.0 %collective-permute-start.12 = (f32[1,2,1,1024]{3,2,1,0:T(1,128)S(1)}, f32[1,2,1,1024]{3,2,1,0:T(1,128)S(1)}, u32[]{:S(2)}, u32[]{:S(2)}) collective-permute-start(f32[1,2,1,1024]{3,2,1,0:T(1,128)S(1)} %get-tuple-element.37), channel_id=1, source_target_pairs={{0,1},{1,2},{2,3},{4,5},{5,6},{6,7},{8,9},{9,10},{10,11},{12,13},{... | collective-permute-start | bytes 24584 | tf_op jit(solution)/shard_map/ppermute | solution.py:16
  95.6 1.2 fusion.47
  96.8 1.7 reshape.320
  98.5 0.1 slice.284
  98.7 1.8 multiply_reduce_fusion.3
  100.6 1.3 pad_maximum_fusion.13
  101.8 7.9 %all_to_all.38 = f32[8,1,2]{2,1,0:T(1,128)S(1)} all-to-all(f32[8,1,2]{2,1,0:T(1,128)S(1)} %broadcast_in_dim.14), channel_id=1, replica_groups=mesh['win_0'=8,'win_1'=8,'win_2'=2,'tile'=4] {'win_2','tile'}, dimensions={0} | all-to-all | bytes 128 | tf_op jit(solution)/shard_map/all_to_all | solution.py:32
  109.8 15.3 %all_to_all.39 = f32[64,1,2]{2,1,0:T(1,128)S(1)} all-to-all(f32[64,1,2]{2,1,0:T(1,128)S(1)} %broadcast_in_dim.15), channel_id=1, replica_groups=mesh['win_0'=8,'win_1'=8,'win_2'=2,'tile'=4] {'win_0','win_1'}, dimensions={0} | all-to-all | bytes 1024 | tf_op jit(solution)/shard_map/all_to_all | solution.py:32
  125.1 0.1 reduce_sum.115
  125.2 0.6 fusion.76
  130.1 0.9 fusion.65
  131.0 4.0 %collective-permute-start.16 = (f32[1,2,32,1024]{3,2,1,0:T(8,128)S(1)}, f32[1,2,32,1024]{3,2,1,0:T(8,128)S(1)}, u32[]{:S(2)}, u32[]{:S(2)}) collective-permute-start(f32[1,2,32,1024]{3,2,1,0:T(8,128)S(1)} %multiply_subtract_fusion.1), channel_id=1, source_target_pairs={{4,0},{8,4},{12,8},{16,12},{20,16},{24,20},{28,24},{32,28},{36,32}... | collective-permute-start | bytes 786440 | tf_op jit(solution)/shard_map/ppermute | solution.py:27
  135.2 1.3 collective-permute-start.13
  136.5 4.0 %collective-permute-start.14 = (f32[1,2,1,1024]{3,2,1,0:T(1,128)S(1)}, f32[1,2,1,1024]{3,2,1,0:T(1,128)S(1)}, u32[]{:S(2)}, u32[]{:S(2)}) collective-permute-start(f32[1,2,1,1024]{3,2,1,0:T(1,128)S(1)} %get-tuple-element.31), channel_id=1, source_target_pairs={{0,1},{1,2},{2,3},{4,5},{5,6},{6,7},{8,9},{9,10},{10,11},{12,13},{... | collective-permute-start | bytes 24584 | tf_op jit(solution)/shard_map/ppermute | solution.py:16
  140.5 0.2 fusion.46
  140.7 2.0 %fusion.1 = f32[32,1,128]{2,1,0:T(1,128)S(1)} fusion(f32[32,128,1]{1,2,0:T(1,128)S(1)} %bitcast.142, s32[32,128]{1,0:T(8,128)S(1)} %bitcast.149), kind=kOutput, calls=%fused_computation.2 | convolution fusion | flops 6815744 | bytes 49152 | tf_op jit(solution)/shard_map/bjc,bc->bj/dot_general | solution.py:83
  142.7 1.5 fusion
  144.2 0.7 copy-done.6
  144.9 1.9 bitcast_multiply_fusion
  146.9 2.7 %collective-permute-start.15 = (f32[1,2,32,1024]{3,2,1,0:T(8,128)}, f32[1,2,32,1024]{3,2,1,0:T(8,128)}, u32[]{:S(2)}, u32[]{:S(2)}) collective-permute-start(f32[1,2,32,1024]{3,2,1,0:T(8,128)} %get-tuple-element.11), channel_id=1, source_target_pairs={{0,4},{4,8},{8,12},{12,16},{16,20},{20,24},{24,28},{28,32},{32,36}... | collective-permute-start | bytes 786440 | tf_op jit(solution)/shard_map/ppermute | solution.py:27
  149.6 1.3 collective-permute-start.17
  150.9 4.0 %collective-permute-start.18 = (f32[1,2,1,1024]{3,2,1,0:T(1,128)S(1)}, f32[1,2,1,1024]{3,2,1,0:T(1,128)S(1)}, u32[]{:S(2)}, u32[]{:S(2)}) collective-permute-start(f32[1,2,1,1024]{3,2,1,0:T(1,128)S(1)} %get-tuple-element.29), channel_id=1, source_target_pairs={{0,1},{1,2},{2,3},{4,5},{5,6},{6,7},{8,9},{9,10},{10,11},{12,13},{... | collective-permute-start | bytes 24584 | tf_op jit(solution)/shard_map/ppermute | solution.py:16
  154.9 1.2 fusion.45
  156.1 1.7 reshape.326
  157.8 0.1 slice.296
  158.0 2.0 %multiply_reduce_fusion.1 = (f32[]{:T(128)}, f32[]{:T(128)}, f32[1,2,32,1024]{3,2,1,0:T(8,128)S(1)}) fusion(f32[1,2,32,1024]{3,2,1,0:T(8,128)S(1)} %multiply_subtract_fusion.1, f32[1,2,32,1024]{3,2,1,0:T(8,128)} %reshape.326, f32[1,2,32,1]{3,2,1,0:T(8,128)S(1)} %slice.297, f32[1,2,32,1023]{3,2,1,0:T(8,128)S(1)} %slice.296, ...), kind=kLoop, calls=%fused_computation.83 | loop fusion | flops 1114110 | bytes 2637832 | tf_op jit(solution)/shard_map/reduce_sum | solution.py:115
  160.0 1.4 pad_maximum_fusion.14
  161.4 7.9 %all_to_all.40 = f32[8,1,2]{2,1,0:T(1,128)S(1)} all-to-all(f32[8,1,2]{2,1,0:T(1,128)S(1)} %broadcast_in_dim.16), channel_id=1, replica_groups=mesh['win_0'=8,'win_1'=8,'win_2'=2,'tile'=4] {'win_2','tile'}, dimensions={0} | all-to-all | bytes 128 | tf_op jit(solution)/shard_map/all_to_all | solution.py:32
  169.3 15.3 %all_to_all.41 = f32[64,1,2]{2,1,0:T(1,128)S(1)} all-to-all(f32[64,1,2]{2,1,0:T(1,128)S(1)} %broadcast_in_dim.17), channel_id=1, replica_groups=mesh['win_0'=8,'win_1'=8,'win_2'=2,'tile'=4] {'win_0','win_1'}, dimensions={0} | all-to-all | bytes 1024 | tf_op jit(solution)/shard_map/all_to_all | solution.py:32
  184.7 0.6 fusion.75
  189.1 0.9 multiply_subtract_fusion
  (74 shorter events, 1.3 us)
Async XLA Ops:
  0.6 19.2 %copy-start.1 = (f32[1,2,32,1024]{3,2,1,0:T(8,128)S(1)}, f32[1,2,32,1024]{3,2,1,0:T(8,128)}, u32[]{:S(2)}) copy-start(f32[1,2,32,1024]{3,2,1,0:T(8,128)} %param.6) | copy-start | bytes 786436
  0.6 19.3 %copy-start.9 = (s32[1,32]{1,0:T(1,128)S(1)}, s32[1,32]{1,0:T(1,128)}, u32[]{:S(2)}) copy-start(s32[1,32]{1,0:T(1,128)} %param.9) | copy-start | bytes 388
  0.7 19.5 %copy-start.10 = (s32[1,32,128]{2,1,0:T(8,128)S(1)}, s32[1,32,128]{2,1,0:T(8,128)}, u32[]{:S(2)}) copy-start(s32[1,32,128]{2,1,0:T(8,128)} %param.10) | copy-start | bytes 49156
  0.7 23.0 %collective-permute-start.3 = (f32[1,2,32,1024]{3,2,1,0:T(8,128)}, f32[1,2,32,1024]{3,2,1,0:T(8,128)S(1)}, u32[]{:S(2)}, u32[]{:S(2)}) collective-permute-start(f32[1,2,32,1024]{3,2,1,0:T(8,128)} %param.7), channel_id=1, source_target_pairs={{4,0},{8,4},{12,8},{16,12},{20,16},{24,20},{28,24},{32,28},{36,32}... | collective-permute-start | bytes 786440 | tf_op jit(solution)/shard_map/ppermute | solution.py:27
  9.6 14.2 %collective-permute-start.4 = (f32[1,2,32,1024]{3,2,1,0:T(8,128)}, f32[1,2,32,1024]{3,2,1,0:T(8,128)S(1)}, u32[]{:S(2)}, u32[]{:S(2)}) collective-permute-start(f32[1,2,32,1024]{3,2,1,0:T(8,128)} %param.6), channel_id=1, source_target_pairs={{4,0},{8,4},{12,8},{16,12},{20,16},{24,20},{28,24},{32,28},{36,32}... | collective-permute-start | bytes 786440 | tf_op jit(solution)/shard_map/ppermute | solution.py:27
  12.4 11.3 %collective-permute-start = (f32[1,2,1,1024]{3,2,1,0:T(1,128)S(1)}, f32[1,2,1,1024]{3,2,1,0:T(1,128)S(1)}, u32[]{:S(2)}, u32[]{:S(2)}) collective-permute-start(f32[1,2,1,1024]{3,2,1,0:T(1,128)S(1)} %get-tuple-element.46), channel_id=1, source_target_pairs={{1,0},{2,1},{3,2},{5,4},{6,5},{7,6},{9,8},{10,9},{11,10},{13,12},{... | collective-permute-start | bytes 24584 | tf_op jit(solution)/shard_map/ppermute | solution.py:19
  13.7 10.0 %collective-permute-start.1 = (f32[1,2,1,1024]{3,2,1,0:T(1,128)S(1)}, f32[1,2,1,1024]{3,2,1,0:T(1,128)S(1)}, u32[]{:S(2)}, u32[]{:S(2)}) collective-permute-start(f32[1,2,1,1024]{3,2,1,0:T(1,128)S(1)} %get-tuple-element.47), channel_id=1, source_target_pairs={{0,1},{1,2},{2,3},{4,5},{5,6},{6,7},{8,9},{9,10},{10,11},{12,13},{... | collective-permute-start | bytes 24584 | tf_op jit(solution)/shard_map/ppermute | solution.py:16
  18.7 3.5 %copy-start.8 = (f32[1,32,128]{2,1,0:T(8,128)S(1)}, f32[1,32,128]{2,1,0:T(8,128)}, u32[]{:S(2)}) copy-start(f32[1,32,128]{2,1,0:T(8,128)} %param.11) | copy-start | bytes 49156
  20.2 3.5 %copy-start = (f32[4,1,2,32,1024]{4,3,2,1,0:T(8,128)S(1)}, f32[4,1,2,32,1024]{4,3,2,1,0:T(8,128)}, u32[]{:S(2)}) copy-start(f32[4,1,2,32,1024]{4,3,2,1,0:T(8,128)} %param.8) | copy-start | bytes 3145732
  24.7 10.5 %copy-start.2 = (f32[1,2,32,1024]{3,2,1,0:T(8,128)S(1)}, f32[1,2,32,1024]{3,2,1,0:T(8,128)}, u32[]{:S(2)}) copy-start(f32[1,2,32,1024]{3,2,1,0:T(8,128)} %param.7) | copy-start | bytes 786436
  24.7 10.5 %collective-permute-start.2 = (f32[1,2,32,1024]{3,2,1,0:T(8,128)}, f32[1,2,32,1024]{3,2,1,0:T(8,128)}, u32[]{:S(2)}, u32[]{:S(2)}) collective-permute-start(f32[1,2,32,1024]{3,2,1,0:T(8,128)} %get-tuple-element.19), channel_id=1, source_target_pairs={{0,4},{4,8},{8,12},{12,16},{16,20},{20,24},{24,28},{28,32},{32,36}... | collective-permute-start | bytes 786440 | tf_op jit(solution)/shard_map/ppermute | solution.py:27
  29.1 6.0 %collective-permute-start.5 = (f32[1,2,1,1024]{3,2,1,0:T(1,128)S(1)}, f32[1,2,1,1024]{3,2,1,0:T(1,128)S(1)}, u32[]{:S(2)}, u32[]{:S(2)}) collective-permute-start(f32[1,2,1,1024]{3,2,1,0:T(1,128)S(1)} %get-tuple-element.44), channel_id=1, source_target_pairs={{1,0},{2,1},{3,2},{5,4},{6,5},{7,6},{9,8},{10,9},{11,10},{13,12},{... | collective-permute-start | bytes 24584 | tf_op jit(solution)/shard_map/ppermute | solution.py:19
  30.4 4.8 %collective-permute-start.6 = (f32[1,2,1,1024]{3,2,1,0:T(1,128)S(1)}, f32[1,2,1,1024]{3,2,1,0:T(1,128)S(1)}, u32[]{:S(2)}, u32[]{:S(2)}) collective-permute-start(f32[1,2,1,1024]{3,2,1,0:T(1,128)S(1)} %get-tuple-element.45), channel_id=1, source_target_pairs={{0,1},{1,2},{2,3},{4,5},{5,6},{6,7},{8,9},{9,10},{10,11},{12,13},{... | collective-permute-start | bytes 24584 | tf_op jit(solution)/shard_map/ppermute | solution.py:16
  71.8 13.2 %collective-permute-start.10 = (f32[1,2,32,1024]{3,2,1,0:T(8,128)S(1)}, f32[1,2,32,1024]{3,2,1,0:T(8,128)S(1)}, u32[]{:S(2)}, u32[]{:S(2)}) collective-permute-start(f32[1,2,32,1024]{3,2,1,0:T(8,128)S(1)} %multiply_subtract_fusion.2), channel_id=1, source_target_pairs={{4,0},{8,4},{12,8},{16,12},{20,16},{24,20},{28,24},{32,28},{36,32}... | collective-permute-start | bytes 786440 | tf_op jit(solution)/shard_map/ppermute | solution.py:27
  75.9 9.0 %collective-permute-start.7 = (f32[1,2,1,1024]{3,2,1,0:T(1,128)S(1)}, f32[1,2,1,1024]{3,2,1,0:T(1,128)S(1)}, u32[]{:S(2)}, u32[]{:S(2)}) collective-permute-start(f32[1,2,1,1024]{3,2,1,0:T(1,128)S(1)} %get-tuple-element.38), channel_id=1, source_target_pairs={{1,0},{2,1},{3,2},{5,4},{6,5},{7,6},{9,8},{10,9},{11,10},{13,12},{... | collective-permute-start | bytes 24584 | tf_op jit(solution)/shard_map/ppermute | solution.py:19
  77.2 7.7 %collective-permute-start.8 = (f32[1,2,1,1024]{3,2,1,0:T(1,128)S(1)}, f32[1,2,1,1024]{3,2,1,0:T(1,128)S(1)}, u32[]{:S(2)}, u32[]{:S(2)}) collective-permute-start(f32[1,2,1,1024]{3,2,1,0:T(1,128)S(1)} %get-tuple-element.39), channel_id=1, source_target_pairs={{0,1},{1,2},{2,3},{4,5},{5,6},{6,7},{8,9},{9,10},{10,11},{12,13},{... | collective-permute-start | bytes 24584 | tf_op jit(solution)/shard_map/ppermute | solution.py:16
  85.0 0.7 copy-start.7
  87.6 11.1 %collective-permute-start.9 = (f32[1,2,32,1024]{3,2,1,0:T(8,128)}, f32[1,2,32,1024]{3,2,1,0:T(8,128)}, u32[]{:S(2)}, u32[]{:S(2)}) collective-permute-start(f32[1,2,32,1024]{3,2,1,0:T(8,128)} %get-tuple-element.15), channel_id=1, source_target_pairs={{0,4},{4,8},{8,12},{12,16},{16,20},{20,24},{24,28},{28,32},{32,36}... | collective-permute-start | bytes 786440 | tf_op jit(solution)/shard_map/ppermute | solution.py:27
  90.3 8.4 %collective-permute-start.11 = (f32[1,2,1,1024]{3,2,1,0:T(1,128)S(1)}, f32[1,2,1,1024]{3,2,1,0:T(1,128)S(1)}, u32[]{:S(2)}, u32[]{:S(2)}) collective-permute-start(f32[1,2,1,1024]{3,2,1,0:T(1,128)S(1)} %get-tuple-element.36), channel_id=1, source_target_pairs={{1,0},{2,1},{3,2},{5,4},{6,5},{7,6},{9,8},{10,9},{11,10},{13,12},{... | collective-permute-start | bytes 24584 | tf_op jit(solution)/shard_map/ppermute | solution.py:19
  91.6 7.1 %collective-permute-start.12 = (f32[1,2,1,1024]{3,2,1,0:T(1,128)S(1)}, f32[1,2,1,1024]{3,2,1,0:T(1,128)S(1)}, u32[]{:S(2)}, u32[]{:S(2)}) collective-permute-start(f32[1,2,1,1024]{3,2,1,0:T(1,128)S(1)} %get-tuple-element.37), channel_id=1, source_target_pairs={{0,1},{1,2},{2,3},{4,5},{5,6},{6,7},{8,9},{9,10},{10,11},{12,13},{... | collective-permute-start | bytes 24584 | tf_op jit(solution)/shard_map/ppermute | solution.py:16
  131.0 13.2 %collective-permute-start.16 = (f32[1,2,32,1024]{3,2,1,0:T(8,128)S(1)}, f32[1,2,32,1024]{3,2,1,0:T(8,128)S(1)}, u32[]{:S(2)}, u32[]{:S(2)}) collective-permute-start(f32[1,2,32,1024]{3,2,1,0:T(8,128)S(1)} %multiply_subtract_fusion.1), channel_id=1, source_target_pairs={{4,0},{8,4},{12,8},{16,12},{20,16},{24,20},{28,24},{32,28},{36,32}... | collective-permute-start | bytes 786440 | tf_op jit(solution)/shard_map/ppermute | solution.py:27
  135.2 9.0 %collective-permute-start.13 = (f32[1,2,1,1024]{3,2,1,0:T(1,128)S(1)}, f32[1,2,1,1024]{3,2,1,0:T(1,128)S(1)}, u32[]{:S(2)}, u32[]{:S(2)}) collective-permute-start(f32[1,2,1,1024]{3,2,1,0:T(1,128)S(1)} %get-tuple-element.30), channel_id=1, source_target_pairs={{1,0},{2,1},{3,2},{5,4},{6,5},{7,6},{9,8},{10,9},{11,10},{13,12},{... | collective-permute-start | bytes 24584 | tf_op jit(solution)/shard_map/ppermute | solution.py:19
  136.5 7.7 %collective-permute-start.14 = (f32[1,2,1,1024]{3,2,1,0:T(1,128)S(1)}, f32[1,2,1,1024]{3,2,1,0:T(1,128)S(1)}, u32[]{:S(2)}, u32[]{:S(2)}) collective-permute-start(f32[1,2,1,1024]{3,2,1,0:T(1,128)S(1)} %get-tuple-element.31), channel_id=1, source_target_pairs={{0,1},{1,2},{2,3},{4,5},{5,6},{6,7},{8,9},{9,10},{10,11},{12,13},{... | collective-permute-start | bytes 24584 | tf_op jit(solution)/shard_map/ppermute | solution.py:16
  140.7 4.2 %copy-start.4 = (f32[1,2,32,1023]{3,2,1,0:T(8,128)S(1)}, f32[1,2,32,1023]{3,2,1,0:T(8,128)}, u32[]{:S(2)}) copy-start(f32[1,2,32,1023]{3,2,1,0:T(8,128)} %get-tuple-element.32) | copy-start | bytes 785668
  140.7 4.2 %copy-start.5 = (f32[1,2,32,1023]{3,2,1,0:T(8,128)S(1)}, f32[1,2,32,1023]{3,2,1,0:T(8,128)}, u32[]{:S(2)}) copy-start(f32[1,2,32,1023]{3,2,1,0:T(8,128)} %get-tuple-element.33) | copy-start | bytes 785668
  144.2 0.7 copy-start.6
  146.9 2.7 %copy-start.3 = (f32[1,2,32,1024]{3,2,1,0:T(8,128)}, f32[1,2,32,1024]{3,2,1,0:T(8,128)S(1)}, u32[]{:S(2)}) copy-start(f32[1,2,32,1024]{3,2,1,0:T(8,128)S(1)} %get-tuple-element.20) | copy-start | bytes 786436
  146.9 11.1 %collective-permute-start.15 = (f32[1,2,32,1024]{3,2,1,0:T(8,128)}, f32[1,2,32,1024]{3,2,1,0:T(8,128)}, u32[]{:S(2)}, u32[]{:S(2)}) collective-permute-start(f32[1,2,32,1024]{3,2,1,0:T(8,128)} %get-tuple-element.11), channel_id=1, source_target_pairs={{0,4},{4,8},{8,12},{12,16},{16,20},{20,24},{24,28},{28,32},{32,36}... | collective-permute-start | bytes 786440 | tf_op jit(solution)/shard_map/ppermute | solution.py:27
  149.6 8.4 %collective-permute-start.17 = (f32[1,2,1,1024]{3,2,1,0:T(1,128)S(1)}, f32[1,2,1,1024]{3,2,1,0:T(1,128)S(1)}, u32[]{:S(2)}, u32[]{:S(2)}) collective-permute-start(f32[1,2,1,1024]{3,2,1,0:T(1,128)S(1)} %get-tuple-element.28), channel_id=1, source_target_pairs={{1,0},{2,1},{3,2},{5,4},{6,5},{7,6},{9,8},{10,9},{11,10},{13,12},{... | collective-permute-start | bytes 24584 | tf_op jit(solution)/shard_map/ppermute | solution.py:19
  150.9 7.1 %collective-permute-start.18 = (f32[1,2,1,1024]{3,2,1,0:T(1,128)S(1)}, f32[1,2,1,1024]{3,2,1,0:T(1,128)S(1)}, u32[]{:S(2)}, u32[]{:S(2)}) collective-permute-start(f32[1,2,1,1024]{3,2,1,0:T(1,128)S(1)} %get-tuple-element.29), channel_id=1, source_target_pairs={{0,1},{1,2},{2,3},{4,5},{5,6},{6,7},{8,9},{9,10},{10,11},{12,13},{... | collective-permute-start | bytes 24584 | tf_op jit(solution)/shard_map/ppermute | solution.py:16
where the time goes:
time: 191 us; the launch traced here: 190 us
  blocking collectives  77.6 us (41%)
  starting transfers between devices  60.2 us (32%)
  other arithmetic  15.9 us (8%)
  matrix products  13.9 us (7%)
  local copies, waits for them, and re-layouts  11.8 us (6%)
  between operations  10.6 us (6%)
    all_to_all x6, blocking collectives, sent_to_all(): lax.all_to_all(jnp.broadcast_to(x[None], (devices, *x.shape)), axis, 0, 0...  77.6 us
    ppermute x7, starting transfers between devices, passed_along(): return lax.ppermute(x, axis, pairs)  28.6 us
    ppermute x6, starting transfers between devices, extended(): lax.ppermute(lax.slice_in_dim(block, block.shape[dim] - width, None, axis...  23.9 us
    ppermute x6, starting transfers between devices, extended(): lax.ppermute(lax.slice_in_dim(block, 0, width, axis=dim), axis, backward)  7.75 us
    dot_general x3, matrix products, observe(): jnp.einsum('bjc,bc->bj', cell_hot, picked, precision=lax.Precision.HIGHEST)  5.99 us
    reduce_sum x3, other arithmetic, two_products(): jnp.sum(vector * vector)  5.65 us
    mul x3, other arithmetic, backward(): coeffs[3] * state  4.68 us
    dot_general x3, matrix products, observe(): jnp.einsum('bjc,bj->bc', cell_hot, weighted, precision=lax.Precision.HIGH...  4.39 us
  transfers between devices with their start and end apart: 19, of which 0 were waited for; matrix products, arithmetic and copies ran while one was open for 11% of the time, Pallas kernels for 0%

commit v1 on v0

v1 whole, which is shorter than its diff:
```python
import jax
import jax.numpy as jnp
from jax import lax
from jax.experimental import pallas as pl
from jax.experimental.pallas import tpu as pltpu
from jax.sharding import PartitionSpec as P

MESH = pl.DeviceIdType.MESH
F32 = jnp.float32
LEV, TY, NX = 2, 32, 1024
BLOCKS = TY // 8
STEPS = 3
SCALE = 1.0 / 16.0
NZ, NYC, NCORE, NT = 8, 8, 2, 4
NWIN = NZ * NYC * NCORE
PAIRS = ((0, 0), (0, 1), (1, 1), (0, 2), (1, 2), (2, 2), (0, 3), (1, 3), (2, 3))
HALO_N, HALO_S, EDGE, STATE, IMAGE, IMAGE_EDGE, ADJ_N, ADJ_S = 0, 1, 2, 3, 5, 7, 8, 9
MESSAGES = 10


def two_sum(a, b):
    s = a + b
    t = s - a
    return s, (a - (s - t)) + (b - t)


def quick_sum(a, b):
    s = a + b
    return s, b - (s - a)


def split(a):
    c = a * 4097.0
    high = c - (c - a)
    return high, a - high


def two_prod_split(a, b, sa, sb):
    p = a * b
    return p, ((sa[0] * sb[0] - p) + sa[0] * sb[1] + sa[1] * sb[0]) + sa[1] * sb[1]


def two_prod(a, b):
    return two_prod_split(a, b, split(a), split(b))


def add2(a, b):
    s, e = two_sum(a[0], b[0])
    return quick_sum(s, e + (a[1] + b[1]))


def neg2(a):
    return -a[0], -a[1]


def sub2(a, b):
    return add2(a, neg2(b))


def mul2(a, b):
    p, e = two_prod(a[0], b[0])
    return quick_sum(p, e + (a[0] * b[1] + a[1] * b[0]))


def div2(a, b):
    zero = jnp.zeros_like(a[0])
    first = a[0] / b[0]
    rest = sub2(a, mul2((first, zero), b))
    second = rest[0] / b[0]
    rest = sub2(rest, mul2((second, zero), b))
    third = rest[0] / b[0]
    return add2(quick_sum(first, second), (third, zero))


def tree2(items):
    while len(items) > 1:
        items = [
            add2(items[i], items[i + 1]) if i + 1 < len(items) else items[i]
            for i in range(0, len(items), 2)
        ]
    return items[0]


def kernel(
    right_hbm,
    weight_hbm,
    coeff_hbm,
    block_hbm,
    pos_hbm,
    obsw_hbm,
    v1,
    v2,
    v3,
    combo,
    v0,
    weight,
    coeff,
    block,
    pos,
    obsw,
    diag,
    edge,
    weight_edge,
    halo_n,
    halo_s,
    next_edge,
    next_weight_edge,
    next_state,
    next_weight,
    image,
    before,
    image_edge,
    before_edge,
    adj_edge,
    adj_n,
    adj_s,
    follow,
    spread,
    gram_high,
    gram_low,
    row_send,
    row_recv,
    local_sem,
    send_sem,
    recv_sem,
    wsend_sem,
    wrecv_sem,
    rsend_sem,
    rrecv_sem,
):
    win = lax.axis_index("win")
    tile = lax.axis_index("tile")
    core = win % 2
    chip_y = (win // 2) % 8
    chip_z = win // 16
    has_prev, has_next = win > 0, win < NWIN - 1
    has_north, has_south = tile > 0, tile < NT - 1
    prev_id, next_id = (win - 1, tile), (win + 1, tile)
    north_id, south_id = (win, tile - 1), (win, tile + 1)
    states = (v0, v1, v2, v3)

    loads = [
        pltpu.make_async_copy(src, dst, local_sem.at[i])
        for i, (src, dst) in enumerate(
            (
                (right_hbm, v0),
                (weight_hbm, weight),
                (coeff_hbm, coeff),
                (block_hbm, block),
                (pos_hbm, pos),
                (obsw_hbm, obsw),
            )
        )
    ]
    for load in loads:
        load.start()

    slot_a = core * NT + tile
    peers_a, peers_b, peers_c = [], [], []
    for i in range(1, NCORE * NT):
        other = (slot_a + i) % (NCORE * NT)
        peers_a.append((win - core + other // NT, other % NT))
    for i in range(1, NYC):
        other = (chip_y + i) % NYC
        peers_b.append((win + 2 * (other - chip_y), tile))
    for i in range(1, NZ):
        other = (chip_z + i) % NZ
        peers_c.append((win + 16 * (other - chip_z), tile))

    barrier = pltpu.get_barrier_semaphore()
    for peer in (*peers_a, *peers_b, *peers_c):
        pl.semaphore_signal(barrier, inc=1, device_id=peer, device_id_type=MESH)

    @pl.when(has_prev)
    def _():
        pl.semaphore_signal(barrier, inc=1, device_id=prev_id, device_id_type=MESH)

    @pl.when(has_next)
    def _():
        pl.semaphore_signal(barrier, inc=1, device_id=next_id, device_id_type=MESH)

    @pl.when(jnp.logical_not(has_north))
    def _():
        halo_n[...] = jnp.zeros_like(halo_n)
        adj_n[...] = jnp.zeros_like(adj_n)

    @pl.when(jnp.logical_not(has_south))
    def _():
        halo_s[...] = jnp.zeros_like(halo_s)
        adj_s[...] = jnp.zeros_like(adj_s)

    @pl.when(jnp.logical_not(has_prev))
    def _():
        before[...] = jnp.zeros_like(before)
        before_edge[...] = jnp.zeros_like(before_edge)

    @pl.when(jnp.logical_not(has_next))
    def _():
        next_edge[...] = jnp.zeros_like(next_edge)
        next_weight_edge[...] = jnp.zeros_like(next_weight_edge)
        next_state[...] = jnp.zeros_like(next_state)
        next_weight[...] = jnp.zeros_like(next_weight)

    for i in range(2):
        loads[i].wait()
    for side, row in ((0, 0), (1, TY - 1)):
        for l in range(LEV):
            edge[0, side, l : l + 1, :] = v0[l, row : row + 1, :]
            weight_edge[side, l : l + 1, :] = weight[l, row : row + 1, :]

    near = jnp.where(has_prev, 1, 0) + jnp.where(has_next, 1, 0)
    pl.semaphore_wait(barrier, len(peers_a) + len(peers_b) + len(peers_c) + near)

    started = []

    def remote(src, dst, send, recv, peer):
        return pltpu.make_async_remote_copy(
            src_ref=src, dst_ref=dst, send_sem=send, recv_sem=recv, device_id=peer, device_id_type=MESH
        )

    def start_if(condition, copies):
        @pl.when(condition)
        def _():
            for copy in copies:
                copy.start()

        started.append((condition, copies))

    def wait_if(condition, copies):
        @pl.when(condition)
        def _():
            for copy in copies:
                copy.wait_recv()

    row_id = lax.broadcasted_iota(jnp.int32, (8, NX), 0)
    first_row, last_row = row_id == 0, row_id == 7

    def for_blocks(body):
        def step(b, _):
            body(b)
            return 0

        lax.fori_loop(0, BLOCKS, step, 0)

    def rows(b):
        return pl.ds(pl.multiple_of(b * 8, 8), 8)

    def vertical(ref, l, b):
        here = ref[l, rows(b), :]
        above = ref[l, rows(jnp.maximum(b - 1, 0)), :]
        below = ref[l, rows(jnp.minimum(b + 1, BLOCKS - 1)), :]
        above = above * jnp.where(b > 0, 1.0, 0.0)
        below = below * jnp.where(b < BLOCKS - 1, 1.0, 0.0)
        north = jnp.where(first_row, pltpu.roll(above, 1, 0), pltpu.roll(here, 1, 0))
        south = jnp.where(last_row, pltpu.roll(below, 7, 0), pltpu.roll(here, 7, 0))
        return north + south

    def gram(index):
        i, j = PAIRS[index]
        zero = jnp.zeros((8, NX), F32)

        def step(n, acc):
            l, b = n // BLOCKS, n % BLOCKS
            x = states[i][l, rows(b), :]
            y = states[j][l, rows(b), :]
            p, e = two_prod(x, y)
            s, f = two_sum(acc[0], p)
            return s, acc[1] + (e + f)

        high, low = lax.fori_loop(0, LEV * BLOCKS, step, (zero, zero))
        parts = [(high[:, c * 128 : (c + 1) * 128], low[:, c * 128 : (c + 1) * 128]) for c in range(8)]
        total = tree2([quick_sum(*part) for part in parts])
        for shift in (4, 2, 1):
            total = add2(total, (pltpu.roll(total[0], shift, 0), pltpu.roll(total[1], shift, 0)))
        gram_high[index : index + 1, :] = total[0][0:1, :]
        gram_low[index : index + 1, :] = total[1][0:1, :]

    def observed_weights():
        pos_t = jnp.swapaxes(pos[...], 0, 1)
        obsw_t = jnp.swapaxes(obsw[...], 0, 1)
        lane = lax.broadcasted_iota(jnp.int32, (128, 128), 1)
        lines = []
        for b in range(32):
            hit = pos_t[:, b : b + 1] == lane
            lines.append(jnp.sum(jnp.where(hit, obsw_t[:, b : b + 1], 0.0), axis=0, keepdims=True))
        per_block = jnp.concatenate(lines, axis=0)
        row = lax.broadcasted_iota(jnp.int32, (LEV * TY, 32), 0)
        for c in range(NX // 128):
            hot = (block[...] == row * (NX // 128) + c).astype(F32)
            out = jnp.dot(hot, per_block, precision=lax.Precision.HIGHEST, preferred_element_type=F32)
            for l in range(LEV):
                diag[l, :, c * 128 : (c + 1) * 128] = out[l * TY : (l + 1) * TY, :]

    for j in range(STEPS):
        v, out = states[j], states[j + 1]
        ssem, rsem = send_sem.at[j], recv_sem.at[j]
        to_south = [remote(edge.at[j, 1], halo_n.at[j], ssem.at[HALO_N], rsem.at[HALO_N], south_id)]
        to_north = [remote(edge.at[j, 0], halo_s.at[j], ssem.at[HALO_S], rsem.at[HALO_S], north_id)]
        back_edge = [remote(edge.at[j], next_edge.at[j], ssem.at[EDGE], rsem.at[EDGE], prev_id)]
        back = [
            remote(v.at[l], next_state.at[j, l], ssem.at[STATE + l], rsem.at[STATE + l], prev_id)
            for l in range(LEV)
        ]
        back_weight, back_weight_edge = [], []
        if j == 0:
            back_weight_edge = [
                remote(weight_edge, next_weight_edge, wsend_sem.at[2], wrecv_sem.at[2], prev_id)
            ]
            back_weight = [
                remote(weight.at[l], next_weight.at[l], wsend_sem.at[l], wrecv_sem.at[l], prev_id)
                for l in range(LEV)
            ]
        ahead = [
            remote(image.at[j, l], before.at[j, l], ssem.at[IMAGE + l], rsem.at[IMAGE + l], next_id)
            for l in range(LEV)
        ]
        ahead_edge = [
            remote(image_edge.at[j], before_edge.at[j], ssem.at[IMAGE_EDGE], rsem.at[IMAGE_EDGE], next_id)
        ]
        adj_to_south = [remote(adj_edge.at[j, 1], adj_n.at[j], ssem.at[ADJ_N], rsem.at[ADJ_N], south_id)]
        adj_to_north = [remote(adj_edge.at[j, 0], adj_s.at[j], ssem.at[ADJ_S], rsem.at[ADJ_S], north_id)]

        start_if(has_south, to_south)
        start_if(has_north, to_north)
        interleaved = [*back_edge, *back_weight_edge]
        for l in range(LEV):
            interleaved.append(back[l])
            interleaved.extend(back_weight[l : l + 1])
        start_if(has_prev, interleaved)

        if j == 0:
            loads[2].wait()
        for l in range(LEV):

            def propagate(b, l=l):
                here = v[l, rows(b), :]
                image[j, l, rows(b), :] = (
                    coeff[0, l, rows(b), :] * here
                    + coeff[1, l, rows(b), :] * vertical(v, l, b)
                    + coeff[2, l, rows(b), :] * pltpu.roll(here, NX - 1, 1)
                    + coeff[3, l, rows(b), :] * pltpu.roll(here, 1, 1)
                )

            for_blocks(propagate)
            start_if(has_next, [ahead[l]])

        wait_if(has_north, to_south)
        wait_if(has_south, to_north)
        for side, row, halo in ((0, 0, halo_n), (1, TY - 1, halo_s)):
            for l in range(LEV):
                image_edge[j, side, l : l + 1, :] = (
                    coeff[1, l, row : row + 1, :] * halo[j, l : l + 1, :]
                )
        start_if(has_next, ahead_edge)
        wait_if(has_next, [*back_edge, *back_weight_edge])
        edge_follow = {}
        for side, row in ((0, 0), (1, TY - 1)):
            for l in range(LEV):
                f = next_weight_edge[side, l : l + 1, :] * (
                    next_edge[j, side, l : l + 1, :]
                    - (image[j, l, row : row + 1, :] + image_edge[j, side, l : l + 1, :])
                )
                edge_follow[side, l] = f
                adj_edge[j, side, l : l + 1, :] = coeff[1, l, row : row + 1, :] * f
        start_if(has_south, adj_to_south)
        start_if(has_north, adj_to_north)

        if j == 0:
            for load in loads[3:]:
                load.wait()
            observed_weights()
        if j == 1:
            for index in (0, 1, 2):
                gram(index)
        if j == 2:
            for index in (3, 4, 5):
                gram(index)

        for l in range(LEV):
            wait_if(has_next, [back[l], *back_weight[l : l + 1]])

            def following(b, l=l):
                f = next_weight[l, rows(b), :] * (next_state[j, l, rows(b), :] - image[j, l, rows(b), :])
                follow[l, rows(b), :] = f
                spread[l, rows(b), :] = coeff[1, l, rows(b), :] * f

            for_blocks(following)
            for side, row in ((0, 0), (1, TY - 1)):
                follow[l, row : row + 1, :] = edge_follow[side, l]
                spread[l, row : row + 1, :] = adj_edge[j, side, l : l + 1, :]

            def adjoint(b, l=l):
                f = follow[l, rows(b), :]
                back_image = (
                    coeff[0, l, rows(b), :] * f
                    + vertical(spread, l, b)
                    + pltpu.roll(coeff[2, l, rows(b), :] * f, 1, 1)
                    + pltpu.roll(coeff[3, l, rows(b), :] * f, NX - 1, 1)
                )
                here = v[l, rows(b), :]
                out[l, rows(b), :] = (
                    weight[l, rows(b), :] * here - back_image + diag[l, rows(b), :] * here
                )

            for_blocks(adjoint)

        wait_if(has_north, adj_to_south)
        wait_if(has_south, adj_to_north)
        wait_if(has_prev, ahead_edge)
        for l in range(LEV):
            wait_if(has_prev, [ahead[l]])

            def finish(b, l=l):
                out[l, rows(b), :] = SCALE * (
                    out[l, rows(b), :] - weight[l, rows(b), :] * before[j, l, rows(b), :]
                )

            for_blocks(finish)
            for side, row, adj in ((0, 0, adj_n), (1, TY - 1, adj_s)):
                e = out[l, row : row + 1, :] - SCALE * (
                    adj[j, l : l + 1, :]
                    + weight[l, row : row + 1, :] * before_edge[j, side, l : l + 1, :]
                )
                out[l, row : row + 1, :] = e
                if j + 1 < STEPS:
                    edge[j + 1, side, l : l + 1, :] = e

    for index in (6, 7, 8):
        gram(index)

    sub = lax.broadcasted_iota(jnp.int32, (16, 128), 0)
    valid = sub < len(PAIRS)
    total = (jnp.where(valid, gram_high[...], 0.0), jnp.where(valid, gram_low[...], 0.0))
    for shift in (64, 32, 16, 8, 4, 2, 1):
        total = add2(total, (pltpu.roll(total[0], shift, 1), pltpu.roll(total[1], shift, 1)))
    lane = lax.broadcasted_iota(jnp.int32, (16, 128), 1)
    packed = jnp.where(lane == sub, total[0], jnp.where(lane == sub + 16, total[1], 0.0))
    line = jnp.sum(packed, axis=0, keepdims=True)
    line_lane = lax.broadcasted_iota(jnp.int32, (1, 128), 1)
    for stage, (mine, peers) in enumerate(((slot_a, peers_a), (chip_y, peers_b), (chip_z, peers_c))):
        row_send[stage] = line
        row_recv[stage, mine] = line
        copies = [
            remote(row_send.at[stage], row_recv.at[stage, mine], rsend_sem.at[stage, i], rrecv_sem.at[stage, i], peer)
            for i, peer in enumerate(peers)
        ]
        for copy in copies:
            copy.start()
        started.append((None, copies))
        for copy in copies:
            copy.wait_recv()
        parts = [row_recv[stage, i] for i in range(8)]
        total = tree2([(part, pltpu.roll(part, 128 - 16, 1)) for part in parts])
        line = jnp.where(
            line_lane < 16, total[0], jnp.where(line_lane < 32, pltpu.roll(total[1], 16, 1), 0.0)
        )

    def value(i, j):
        at = PAIRS.index((min(i, j), max(i, j)))
        return tuple(
            jnp.broadcast_to(line[:, at + off : at + off + 1], (8, 128)) for off in (0, 16)
        )

    a = [[value(i, n + 1) for n in range(3)] + [value(i, 0)] for i in range(3)]
    for pivot in range(2):
        for i in range(pivot + 1, 3):
            factor = div2(a[i][pivot], a[pivot][pivot])
            for n in range(pivot + 1, 4):
                a[i][n] = sub2(a[i][n], mul2(factor, a[pivot][n]))
    c2 = div2(a[2][3], a[2][2])
    c1 = div2(sub2(a[1][3], mul2(a[1][2], c2)), a[1][1])
    c0 = div2(sub2(sub2(a[0][3], mul2(a[0][1], c1)), mul2(a[0][2], c2)), a[0][0])
    for i, c in enumerate((c0, c1, c2)):
        combo[i] = c[0]

    for condition, copies in started:

        def drain(copies=copies):
            for copy in copies:
                copy.wait_send()

        if condition is None:
            drain()
        else:
            pl.when(condition)(drain)


def on_device(right_side, error_weight, coeffs, obs_block, obs_pos, obs_weight):
    shape = (LEV, TY, NX)
    right = right_side.reshape(shape)
    vmem, hbm = pltpu.VMEM, pltpu.HBM
    state = jax.ShapeDtypeStruct(shape, F32)
    line = (STEPS, 2, LEV, NX)
    scratch = [
        vmem(shape, F32),
        vmem(shape, F32),
        vmem((4, *shape), F32),
        vmem((1, 32), jnp.int32),
        vmem((32, 128), jnp.int32),
        vmem((32, 128), F32),
        vmem(shape, F32),
        vmem(line, F32),
        vmem(line[1:], F32),
        vmem((STEPS, LEV, NX), F32),
        vmem((STEPS, LEV, NX), F32),
        vmem(line, F32),
        vmem(line[1:], F32),
        vmem((STEPS, *shape), F32),
        vmem(shape, F32),
        vmem((STEPS, *shape), F32),
        vmem((STEPS, *shape), F32),
        vmem(line, F32),
        vmem(line, F32),
        vmem(line, F32),
        vmem((STEPS, LEV, NX), F32),
        vmem((STEPS, LEV, NX), F32),
        vmem(shape, F32),
        vmem(shape, F32),
        vmem((16, 128), F32),
        vmem((16, 128), F32),
        vmem((3, 1, 128), F32),
        vmem((3, 8, 1, 128), F32),
        pltpu.SemaphoreType.DMA((6,)),
        pltpu.SemaphoreType.DMA((STEPS, MESSAGES)),
        pltpu.SemaphoreType.DMA((STEPS, MESSAGES)),
        pltpu.SemaphoreType.DMA((3,)),
        pltpu.SemaphoreType.DMA((3,)),
        pltpu.SemaphoreType.DMA((3, 7)),
        pltpu.SemaphoreType.DMA((3, 7)),
    ]
    v1, v2, v3, combo = pl.pallas_call(
        kernel,
        out_shape=(state, state, state, jax.ShapeDtypeStruct((3, 8, 128), F32)),
        in_specs=[pl.BlockSpec(memory_space=hbm)] * 6,
        out_specs=(pl.BlockSpec(memory_space=vmem),) * 4,
        scratch_shapes=scratch,
        compiler_params=pltpu.CompilerParams(collective_id=0, has_side_effects=True),
        name="krylov",
    )(
        right,
        error_weight.reshape(shape),
        coeffs.reshape(4, *shape),
        obs_block,
        obs_pos.reshape(32, 128),
        obs_weight.reshape(32, 128),
    )
    c0, c1, c2 = (combo[i, 0, 0] for i in range(3))
    solution_field = SCALE * (c0 * right + c1 * v1 + c2 * v2)
    residual = right - c0 * v1 - c1 * v2 - c2 * v3
    return solution_field[None], residual[None]


def solution(mesh):
    in_specs = (
        P("win", None, "tile", None),
        P("win", None, "tile", None),
        P(None, "win", None, "tile", None),
        P("win", "tile"),
        P("win", "tile", None),
        P("win", "tile", None),
    )
    out_specs = (P("win", None, "tile", None), P("win", None, "tile", None))
    return jax.shard_map(on_device, mesh=mesh, in_specs=in_specs, out_specs=out_specs, check_vma=False)
```

time: 191 us -> 58.9 us (0.31)
  blocking collectives: 77.6 us -> 0 us
  starting transfers between devices: 60.2 us -> 0 us
  Pallas kernels: 0 us -> 52.1 us
  matrix products: 13.9 us -> 0 us
  other arithmetic: 15.9 us -> 3.85 us
  local copies, waits for them, and re-layouts: 11.8 us -> 1.28 us
  between operations: 10.6 us -> 0.65 us
    all_to_all x6 -> x0, blocking collectives: 77.6 us -> none  [sent_to_all(): lax.all_to_all(jnp.broadcast_to(x[None], (devices, *x.shape)), axis, 0, 0...]
    ppermute x19 -> x0, starting transfers between devices: 60.2 us -> none  [the longest x7 28.6 us: passed_along(): return lax.ppermute(x, axis, pairs)]
    pallas_call x0 -> x1, Pallas kernels: none -> 52.1 us  [on_device(): pl.pallas_call(kernel, out_shape=(state, state, state, jax.ShapeDtypeStru...]
    dot_general x12 -> x0, matrix products: 13.9 us -> none  [the longest x3 5.99 us: observe(): jnp.einsum('bjc,bc->bj', cell_hot, picked, precision=lax.Precision.HIGHEST)]
    reduce_sum x9 -> x0, other arithmetic: 5.98 us -> none  [the longest x3 5.65 us: two_products(): jnp.sum(vector * vector)]
    mul x9 -> x0, other arithmetic: 4.86 us -> none  [the longest x3 4.68 us: backward(): coeffs[3] * state]
    reshape x6 -> x0, local copies, waits for them, and re-layouts: 4.53 us -> none  [the longest x3 3.44 us: observe(): return spread.reshape(state.shape)]
    slice x24 -> x1, local copies, waits for them, and re-layouts: 5.74 us -> 1.27 us  [on_device(): c0, c1, c2 = (combo[i, 0, 0] for i in range(3))]
  transfers between devices with their start and end apart: 19 -> 0, of which waited for: 0 -> 0; matrix products, arithmetic and copies ran while one was open for 11% -> 0% of each run, Pallas kernels for 0% -> 0%
where the time goes in v1:
time: 58.9 us; the launch traced here: 57.9 us
  Pallas kernels  52.1 us (88%)
  other arithmetic  3.85 us (7%)
  local copies, waits for them, and re-layouts  1.28 us (2%)
  between operations  0.65 us (1%)
    pallas_call x1, Pallas kernels, on_device(): pl.pallas_call(kernel, out_shape=(state, state, state, jax.ShapeDtypeStru...  52.1 us
    broadcast_in_dim x1, other arithmetic, on_device(): return (solution_field[None], residual[None])  3.85 us
    slice x1, local copies, waits for them, and re-layouts, on_device(): c0, c1, c2 = (combo[i, 0, 0] for i in range(3))  1.27 us

profile of v1, /device:TPU:1, one launch (start us, length us, event | category | flops | bytes accessed | tf_op | source)
XLA Modules:
  0.0 57.9 jit_solution(15885227440932140668)
XLA Ops:
  0.6 0.0 copy-start
  0.6 52.1 %krylov.1 = (f32[2,32,1024]{2,1,0:T(8,128)}, f32[2,32,1024]{2,1,0:T(8,128)}, f32[2,32,1024]{2,1,0:T(8,128)}, f32[3,8,128]{2,1,0:T(8,128)}) custom-call(f32[2,32,1024]{2,1,0:T(8,128)} %bitcast.15, f32[2,32,1024]{2,1,0:T(8,128)} %bitcast.16, f32[4,2,32,1024]{3,2,1,0:T(8,128)} %bitcast.14, s32[1,32]{1,0:T(1,128)} %block_hbm.1, s32[32,128]{1,0:T(8,128)} %bitcast.17, ...), custom_call_target="tpu_custom_call" | custom-call | tf_op jit(solution)/shard_map/krylov/pallas_call | solution.py:531
  52.8 1.3 %fusion = (f32[1,1,1]{2,1,0:T(1,128)}, f32[1,1,1]{2,1,0:T(1,128)}, f32[1,1,1]{2,1,0:T(1,128)}) fusion(f32[3,8,128]{2,1,0:T(8,128)} %get-tuple-element.6), kind=kLoop, calls=%fused_computation.2 | loop fusion | bytes 24 | tf_op jit(solution)/shard_map/slice | solution.py:547
  54.0 0.0 copy-done
  54.0 3.9 %subtract_bitcast_fusion = (f32[1,2,32,1024]{3,2,1,0:T(8,128)}, f32[1,2,32,1024]{3,2,1,0:T(8,128)}) fusion(f32[2,32,1024]{2,1,0:T(8,128)} %get-tuple-element.9, f32[2,32,1024]{2,1,0:T(8,128)} %get-tuple-element.8, f32[2,32,1024]{2,1,0:T(8,128)} %get-tuple-element.7, f32[]{:T(128)} %bitcast.7, f32[]{:T(128)} %bitcast.6, f32[]{:T(128)} %bitcast.5, ...), kind=kLoop, calls=%fused_computation | loop fusion | flops 786432 | bytes 1572876 | tf_op jit(solution)/shard_map/broadcast_in_dim | solution.py:550
Async XLA Ops:
  0.6 53.4 %copy-start = (f32[1,2,32,1024]{3,2,1,0:T(8,128)S(1)}, f32[1,2,32,1024]{3,2,1,0:T(8,128)}, u32[]{:S(2)}) copy-start(f32[1,2,32,1024]{3,2,1,0:T(8,128)} %param.6) | copy-start | bytes 786436

commit v2 on v1

v2 whole, which is shorter than its diff:
```python
import jax
import jax.numpy as jnp
from jax import lax
from jax.experimental import pallas as pl
from jax.experimental.pallas import tpu as pltpu
from jax.sharding import PartitionSpec as P

MESH = pl.DeviceIdType.MESH
F32 = jnp.float32
LEV, TY, NX = 2, 32, 1024
BLOCKS = TY // 8
STEPS = 3
SCALE = 1.0 / 16.0
NZ, NYC, NCORE, NT = 8, 8, 2, 4
NWIN = NZ * NYC * NCORE
PAIRS = ((0, 0), (0, 1), (1, 1), (0, 2), (1, 2), (2, 2), (0, 3), (1, 3), (2, 3))
HALO_N, HALO_S, EDGE, STATE, IMAGE, IMAGE_EDGE, ADJ_N, ADJ_S = range(8)
MESSAGES = 8
ROWS = ((0, 0), (1, TY - 1))


def two_sum(a, b):
    s = a + b
    t = s - a
    return s, (a - (s - t)) + (b - t)


def quick_sum(a, b):
    s = a + b
    return s, b - (s - a)


def split(a):
    c = a * 4097.0
    high = c - (c - a)
    return high, a - high


def two_prod_split(a, b, sa, sb):
    p = a * b
    return p, ((sa[0] * sb[0] - p) + sa[0] * sb[1] + sa[1] * sb[0]) + sa[1] * sb[1]


def two_prod(a, b):
    return two_prod_split(a, b, split(a), split(b))


def add2(a, b):
    s, e = two_sum(a[0], b[0])
    return quick_sum(s, e + (a[1] + b[1]))


def neg2(a):
    return -a[0], -a[1]


def sub2(a, b):
    return add2(a, neg2(b))


def mul2(a, b):
    p, e = two_prod(a[0], b[0])
    return quick_sum(p, e + (a[0] * b[1] + a[1] * b[0]))


def div2(a, b):
    zero = jnp.zeros_like(a[0])
    first = a[0] / b[0]
    rest = sub2(a, mul2((first, zero), b))
    return quick_sum(first, rest[0] / b[0])


def tree2(items):
    while len(items) > 1:
        items = [
            add2(items[i], items[i + 1]) if i + 1 < len(items) else items[i]
            for i in range(0, len(items), 2)
        ]
    return items[0]


def rolled(pair, shift, axis):
    return pltpu.roll(pair[0], shift, axis), pltpu.roll(pair[1], shift, axis)


def kernel(
    right_hbm,
    weight_hbm,
    coeff_hbm,
    block_hbm,
    pos_hbm,
    obsw_hbm,
    solution_out,
    residual_out,
    v0,
    v1,
    v2,
    v3,
    weight,
    coeff,
    block,
    pos,
    obsw,
    diag,
    edge,
    weight_edge,
    halo_n,
    halo_s,
    next_edge,
    next_weight_edge,
    next_state,
    next_weight,
    image,
    before,
    image_edge,
    before_edge,
    adj_edge,
    adj_n,
    adj_s,
    follow,
    spread,
    gram_high,
    gram_low,
    row_send,
    row_recv,
    local_sem,
    send_sem,
    recv_sem,
    wsend_sem,
    wrecv_sem,
    rsend_sem,
    rrecv_sem,
    known_sem,
):
    win = lax.axis_index("win")
    tile = lax.axis_index("tile")
    core = win % 2
    chip_y = (win // 2) % 8
    chip_z = win // 16
    has_prev, has_next = win > 0, win < NWIN - 1
    has_north, has_south = tile > 0, tile < NT - 1
    prev_id, next_id = (win - 1, tile), (win + 1, tile)
    north_id, south_id = (win, tile - 1), (win, tile + 1)
    states = (v0, v1, v2, v3)

    loads = [
        pltpu.make_async_copy(src, dst, local_sem.at[i])
        for i, (src, dst) in enumerate(
            (
                (right_hbm, v0),
                (weight_hbm, weight),
                (coeff_hbm, coeff),
                (block_hbm, block),
                (pos_hbm, pos),
                (obsw_hbm, obsw),
            )
        )
    ]
    for load in loads:
        load.start()

    def along_y(by):
        return (win + 2 * ((chip_y + by) % NYC - chip_y), tile)

    def along_z(by, other_core=False):
        start = win + 1 - 2 * core if other_core else win
        return (start + 16 * ((chip_z + by) % NZ - chip_z), tile)

    slot_a = core * NT + tile
    near = [
        (win - core + ((slot_a + i) % 8) // NT, ((slot_a + i) % 8) % NT) for i in range(1, NCORE * NT)
    ]
    near += [along_y(1), along_y(-1)]
    near += [along_z(by, other) for by in (1, -1) for other in (False, True)]

    def signal(semaphore, peer):
        pl.semaphore_signal(semaphore, inc=1, device_id=peer, device_id_type=MESH)

    barrier = pltpu.get_barrier_semaphore()

    @pl.when(has_prev)
    def _():
        signal(barrier, prev_id)

    @pl.when(has_next)
    def _():
        signal(barrier, next_id)

    for peer in near:
        signal(barrier, peer)

    for i in range(2):
        loads[i].wait()
    for side, row in ROWS:
        for l in range(LEV):
            edge[0, l, side] = v0[l, row : row + 1, :]
            weight_edge[l, side] = weight[l, row : row + 1, :]

    pl.semaphore_wait(barrier, len(near) + jnp.where(has_prev, 1, 0) + jnp.where(has_next, 1, 0))

    started = []

    def remote(src, dst, send, recv, peer):
        return pltpu.make_async_remote_copy(
            src_ref=src, dst_ref=dst, send_sem=send, recv_sem=recv, device_id=peer, device_id_type=MESH
        )

    def start_if(condition, copies):
        @pl.when(condition)
        def _():
            for copy in copies:
                copy.start()

        started.append((condition, copies))

    def wait_if(condition, copies):
        @pl.when(condition)
        def _():
            for copy in copies:
                copy.wait_recv()

    def message(kind, j, l):
        src, dst, peer = {
            HALO_N: (edge.at[j, l, 1], halo_n.at[j, l], south_id),
            HALO_S: (edge.at[j, l, 0], halo_s.at[j, l], north_id),
            EDGE: (edge.at[j, l], next_edge.at[j, l], prev_id),
            STATE: (states[j].at[l], next_state.at[j, l], prev_id),
            IMAGE: (image.at[j, l], before.at[j, l], next_id),
            IMAGE_EDGE: (image_edge.at[j, l], before_edge.at[j, l], next_id),
            ADJ_N: (adj_edge.at[j, l, 1], adj_n.at[j, l], south_id),
            ADJ_S: (adj_edge.at[j, l, 0], adj_s.at[j, l], north_id),
        }[kind]
        return remote(src, dst, send_sem.at[j, l, kind], recv_sem.at[j, l, kind], peer)

    def weight_messages(l):
        return [
            remote(weight_edge.at[l], next_weight_edge.at[l], wsend_sem.at[l, 0], wrecv_sem.at[l, 0], prev_id),
            remote(weight.at[l], next_weight.at[l], wsend_sem.at[l, 1], wrecv_sem.at[l, 1], prev_id),
        ]

    row_id = lax.broadcasted_iota(jnp.int32, (8, NX), 0)
    first_row, last_row = row_id == 0, row_id == 7

    def rows(b):
        return slice(8 * b, 8 * b + 8)

    def vertical(ref, l, b):
        here = ref[l, rows(b), :]
        above = pltpu.roll(ref[l, rows(b - 1), :], 1, 0) if b > 0 else 0.0
        below = pltpu.roll(ref[l, rows(b + 1), :], 7, 0) if b < BLOCKS - 1 else 0.0
        north = jnp.where(first_row, above, pltpu.roll(here, 1, 0))
        south = jnp.where(last_row, below, pltpu.roll(here, 7, 0))
        return north + south

    def send_and_propagate(j, l):
        v = states[j]
        start_if(has_south, [message(HALO_N, j, l)])
        start_if(has_north, [message(HALO_S, j, l)])
        back = [message(EDGE, j, l), message(STATE, j, l)]
        if j == 0:
            small, large = weight_messages(l)
            back = [back[0], small, back[1], large]
        start_if(has_prev, back)
        if j == 0 and l == 0:
            loads[2].wait()
        for b in range(BLOCKS):
            here = v[l, rows(b), :]
            image[j, l, rows(b), :] = (
                coeff[0, l, rows(b), :] * here
                + coeff[1, l, rows(b), :] * vertical(v, l, b)
                + coeff[2, l, rows(b), :] * pltpu.roll(here, NX - 1, 1)
                + coeff[3, l, rows(b), :] * pltpu.roll(here, 1, 1)
            )
        start_if(has_next, [message(IMAGE, j, l)])

    edge_follow = {}

    def exchange_edges(j, l):
        wait_if(has_north, [message(HALO_N, j, l)])
        wait_if(has_south, [message(HALO_S, j, l)])
        for side, row in ROWS:
            halo = (halo_n, halo_s)[side]
            image_edge[j, l, side] = coeff[1, l, row : row + 1, :] * halo[j, l]
        start_if(has_next, [message(IMAGE_EDGE, j, l)])
        wait_if(has_next, [message(EDGE, j, l), *(weight_messages(l)[:1] if j == 0 else [])])
        for side, row in ROWS:
            f = next_weight_edge[l, side] * (
                next_edge[j, l, side] - (image[j, l, row : row + 1, :] + image_edge[j, l, side])
            )
            edge_follow[j, l, side] = f
            adj_edge[j, l, side] = coeff[1, l, row : row + 1, :] * f
        start_if(has_south, [message(ADJ_N, j, l)])
        start_if(has_north, [message(ADJ_S, j, l)])

    def complete(j, l):
        v, out = states[j], states[j + 1]
        wait_if(has_next, [message(STATE, j, l), *(weight_messages(l)[1:] if j == 0 else [])])
        for b in range(BLOCKS):
            f = next_weight[l, rows(b), :] * (next_state[j, l, rows(b), :] - image[j, l, rows(b), :])
            follow[l, rows(b), :] = f
            spread[l, rows(b), :] = coeff[1, l, rows(b), :] * f
        for side, row in ROWS:
            follow[l, row : row + 1, :] = edge_follow[j, l, side]
            spread[l, row : row + 1, :] = adj_edge[j, l, side]
        for b in range(BLOCKS):
            f = follow[l, rows(b), :]
            back_image = (
                coeff[0, l, rows(b), :] * f
                + vertical(spread, l, b)
                + pltpu.roll(coeff[2, l, rows(b), :] * f, 1, 1)
                + pltpu.roll(coeff[3, l, rows(b), :] * f, NX - 1, 1)
            )
            here = v[l, rows(b), :]
            out[l, rows(b), :] = weight[l, rows(b), :] * here - back_image + diag[l, rows(b), :] * here
        wait_if(has_north, [message(ADJ_N, j, l)])
        wait_if(has_south, [message(ADJ_S, j, l)])
        wait_if(has_prev, [message(IMAGE_EDGE, j, l), message(IMAGE, j, l)])
        for b in range(BLOCKS):
            out[l, rows(b), :] = SCALE * (
                out[l, rows(b), :] - weight[l, rows(b), :] * before[j, l, rows(b), :]
            )
        for side, row in ROWS:
            adj = (adj_n, adj_s)[side]
            e = out[l, row : row + 1, :] - SCALE * (
                adj[j, l] + weight[l, row : row + 1, :] * before_edge[j, l, side]
            )
            out[l, row : row + 1, :] = e
            if j + 1 < STEPS:
                edge[j + 1, l, side] = e

    def gram(group, l):
        indices = range(3 * group, 3 * group + 3)
        zero = jnp.zeros((8, 128), F32)

        def step(b, acc):
            acc = list(acc)
            at = pl.ds(pl.multiple_of(b * 8, 8), 8)
            for c in range(NX // 128):
                parts = {}
                for index in indices:
                    for s in PAIRS[index]:
                        if s not in parts:
                            x = states[s][l, at, c * 128 : (c + 1) * 128]
                            parts[s] = (x, split(x))
                for n, index in enumerate(indices):
                    i, k = PAIRS[index]
                    p, e = two_prod_split(parts[i][0], parts[k][0], parts[i][1], parts[k][1])
                    s, f = two_sum(acc[2 * n], p)
                    acc[2 * n], acc[2 * n + 1] = s, acc[2 * n + 1] + (e + f)
            return tuple(acc)

        acc = lax.fori_loop(0, BLOCKS, step, (zero,) * 6)
        for n, index in enumerate(indices):
            part = quick_sum(acc[2 * n], acc[2 * n + 1])
            if l > 0:
                part = add2(part, (gram_high[index], gram_low[index]))
            gram_high[index], gram_low[index] = part

    def over_rows(index):
        total = (gram_high[index], gram_low[index])
        for shift in (4, 2, 1):
            total = add2(total, rolled(total, shift, 0))
        return total[0][0:1, :], total[1][0:1, :]

    def observed_weights():
        pos_t = jnp.swapaxes(pos[...], 0, 1)
        obsw_t = jnp.swapaxes(obsw[...], 0, 1)
        lane = lax.broadcasted_iota(jnp.int32, (128, 128), 1)
        lines = []
        for b in range(32):
            hit = pos_t[:, b : b + 1] == lane
            lines.append(jnp.sum(jnp.where(hit, obsw_t[:, b : b + 1], 0.0), axis=0, keepdims=True))
        per_block = jnp.concatenate(lines, axis=0)
        row = lax.broadcasted_iota(jnp.int32, (LEV * TY, 32), 0)
        for c in range(NX // 128):
            hot = (block[...] == row * (NX // 128) + c).astype(F32)
            out = jnp.dot(hot, per_block, precision=lax.Precision.HIGHEST, preferred_element_type=F32)
            for l in range(LEV):
                diag[l, :, c * 128 : (c + 1) * 128] = out[l * TY : (l + 1) * TY, :]

    def zeros(*refs):
        for ref in refs:
            ref[...] = jnp.zeros_like(ref)

    for l in range(LEV):
        send_and_propagate(0, l)
    for at, move in enumerate((along_y, along_z)):
        for by in (1, -1):
            signal(known_sem.at[at, 0], move(by))
    pl.when(jnp.logical_not(has_north))(lambda: zeros(halo_n, adj_n))
    pl.when(jnp.logical_not(has_south))(lambda: zeros(halo_s, adj_s))
    pl.when(jnp.logical_not(has_prev))(lambda: zeros(before, before_edge))
    pl.when(jnp.logical_not(has_next))(lambda: zeros(next_edge, next_weight_edge, next_state, next_weight))
    for load in loads[3:]:
        load.wait()
    observed_weights()
    for at, move in enumerate((along_y, along_z)):
        pl.semaphore_wait(known_sem.at[at, 0], 2)
        for by in (2, -2):
            signal(known_sem.at[at, 1], move(by))
    for l in range(LEV):
        exchange_edges(0, l)
    for j in range(STEPS):
        for l in range(LEV):
            complete(j, l)
            if j + 1 < STEPS:
                send_and_propagate(j + 1, l)
            else:
                gram(2, l)
        if j + 1 < STEPS:
            if j == 0:
                for at in range(2):
                    pl.semaphore_wait(known_sem.at[at, 1], 2)
            for l in range(LEV):
                gram(j, l)
            for l in range(LEV):
                exchange_edges(j + 1, l)

    lines = [over_rows(index) for index in range(len(PAIRS))]
    blank = jnp.zeros((16 - len(PAIRS), 128), F32)
    stacked = jnp.concatenate([*(x for x, _ in lines), blank, *(x for _, x in lines), blank], axis=0)
    turned = jnp.swapaxes(jnp.concatenate([stacked, jnp.zeros((96, 128), F32)], axis=0), 0, 1)
    pieces = [turned[8 * i : 8 * i + 8, :] for i in range(16)]
    total = tree2([(x, pltpu.roll(x, 128 - 16, 1)) for x in pieces])
    for shift in (4, 2, 1):
        total = add2(total, rolled(total, shift, 0))
    lane = lax.broadcasted_iota(jnp.int32, (1, 128), 1)

    def packed(pair):
        return jnp.where(lane < 16, pair[0], jnp.where(lane < 32, pltpu.roll(pair[1], 16, 1), 0.0))

    line = packed((total[0][0:1, :], total[1][0:1, :]))

    def received(stage):
        parts = [row_recv[stage, i] for i in range(8)]
        return tree2([(x, pltpu.roll(x, 128 - 16, 1)) for x in parts])

    def to_x(i, other):
        return remote(
            row_send.at[0], row_recv.at[0, i], rsend_sem.at[0, other], rrecv_sem.at[0, i], (win - core + 1, other)
        )

    def to_y(by):
        return remote(
            row_send.at[1], row_recv.at[1, chip_y], rsend_sem.at[1, by], rrecv_sem.at[1, by], along_y(by)
        )

    def to_z(by, other_core):
        at = by + 8 * other_core
        return remote(
            row_send.at[2], row_recv.at[2, chip_z], rsend_sem.at[2, at], rrecv_sem.at[2, at], along_z(by, other_core)
        )

    is_second = core == 1
    row_send[0] = line
    for other in range(NT):
        condition = jnp.logical_or(core == 0, tile != other)
        start_if(condition, [to_x(slot_a, other)])

    @pl.when(is_second)
    def _():
        row_recv[0, slot_a] = line
        for i in range(NCORE * NT):

            @pl.when(slot_a != i)
            def _(i=i):
                to_x(i, 0).wait_recv()

        mine = packed(received(0))
        row_send[1] = mine
        row_recv[1, chip_y] = mine
        for by in range(1, NYC):
            to_y(by).start()
        for by in range(1, NYC):
            to_y(by).wait_recv()
        mine = packed(received(1))
        row_send[2] = mine
        row_recv[2, chip_z] = mine
        for by in range(1, NZ):
            to_z(by, True).start()
            to_z(by, False).start()
        to_z(0, True).start()
        for by in range(1, NZ):
            to_z(by, False).wait_recv()

    @pl.when(jnp.logical_not(is_second))
    def _():
        for by in range(NZ):
            to_z(by, True).wait_recv()

    total = received(2)
    line = packed(total)

    def value(i, j):
        at = PAIRS.index((min(i, j), max(i, j)))
        return tuple(jnp.broadcast_to(line[:, at + off : at + off + 1], (8, 128)) for off in (0, 16))

    a = [[value(i, n + 1) for n in range(3)] + [value(i, 0)] for i in range(3)]
    for pivot in range(2):
        for i in range(pivot + 1, 3):
            factor = div2(a[i][pivot], a[pivot][pivot])
            for n in range(pivot + 1, 4):
                a[i][n] = sub2(a[i][n], mul2(factor, a[pivot][n]))
    c2 = div2(a[2][3], a[2][2])
    c1 = div2(sub2(a[1][3], mul2(a[1][2], c2)), a[1][1])
    c0 = div2(sub2(sub2(a[0][3], mul2(a[0][1], c1)), mul2(a[0][2], c2)), a[0][0])
    combo = [jnp.concatenate([c[0]] * (NX // 128), axis=1) for c in (c0, c1, c2)]
    for l in range(LEV):
        for b in range(BLOCKS):
            at = (l, rows(b), slice(None))
            u0, u1, u2, u3 = (s[at] for s in states)
            solution_out[0, l, rows(b), :] = SCALE * (combo[0] * u0 + combo[1] * u1 + combo[2] * u2)
            residual_out[0, l, rows(b), :] = u0 - combo[0] * u1 - combo[1] * u2 - combo[2] * u3

    for condition, copies in started:

        @pl.when(condition)
        def _(copies=copies):
            for copy in copies:
                copy.wait_send()

    @pl.when(is_second)
    def _():
        for by in range(1, NYC):
            to_y(by).wait_send()
        for by in range(1, NZ):
            to_z(by, True).wait_send()
            to_z(by, False).wait_send()
        to_z(0, True).wait_send()


def on_device(right_side, error_weight, coeffs, obs_block, obs_pos, obs_weight):
    shape = (LEV, TY, NX)
    vmem, hbm = pltpu.VMEM, pltpu.HBM
    line = (STEPS, LEV, 2, 1, NX)
    half = (STEPS, LEV, 1, NX)
    scratch = [
        vmem(shape, F32),
        vmem(shape, F32),
        vmem(shape, F32),
        vmem(shape, F32),
        vmem(shape, F32),
        vmem((4, *shape), F32),
        vmem((1, 32), jnp.int32),
        vmem((32, 128), jnp.int32),
        vmem((32, 128), F32),
        vmem(shape, F32),
        vmem(line, F32),
        vmem(line[1:], F32),
        vmem(half, F32),
        vmem(half, F32),
        vmem(line, F32),
        vmem(line[1:], F32),
        vmem((STEPS, *shape), F32),
        vmem(shape, F32),
        vmem((STEPS, *shape), F32),
        vmem((STEPS, *shape), F32),
        vmem(line, F32),
        vmem(line, F32),
        vmem(line, F32),
        vmem(half, F32),
        vmem(half, F32),
        vmem(shape, F32),
        vmem(shape, F32),
        vmem((len(PAIRS), 8, 128), F32),
        vmem((len(PAIRS), 8, 128), F32),
        vmem((3, 1, 128), F32),
        vmem((3, 8, 1, 128), F32),
        pltpu.SemaphoreType.DMA((6,)),
        pltpu.SemaphoreType.DMA((STEPS, LEV, MESSAGES)),
        pltpu.SemaphoreType.DMA((STEPS, LEV, MESSAGES)),
        pltpu.SemaphoreType.DMA((LEV, 2)),
        pltpu.SemaphoreType.DMA((LEV, 2)),
        pltpu.SemaphoreType.DMA((3, 16)),
        pltpu.SemaphoreType.DMA((3, 16)),
        pltpu.SemaphoreType.REGULAR((2, 2)),
    ]
    return pl.pallas_call(
        kernel,
        out_shape=(pltpu.VMEM((1, *shape), F32), pltpu.VMEM((1, *shape), F32)),
        in_specs=[pl.BlockSpec(memory_space=hbm)] * 6,
        out_specs=(pl.BlockSpec(memory_space=vmem),) * 2,
        scratch_shapes=scratch,
        compiler_params=pltpu.CompilerParams(collective_id=0, has_side_effects=True),
        name="krylov",
    )(
        right_side.reshape(shape),
        error_weight.reshape(shape),
        coeffs.reshape(4, *shape),
        obs_block,
        obs_pos.reshape(32, 128),
        obs_weight.reshape(32, 128),
    )


def solution(mesh):
    in_specs = (
        P("win", None, "tile", None),
        P("win", None, "tile", None),
        P(None, "win", None, "tile", None),
        P("win", "tile"),
        P("win", "tile", None),
        P("win", "tile", None),
    )
    out_specs = (P("win", None, "tile", None), P("win", None, "tile", None))
    return jax.shard_map(on_device, mesh=mesh, in_specs=in_specs, out_specs=out_specs, check_vma=False)
```

time: 58.9 us -> 49.4 us (0.84); the launches traced: 57.9 us -> 49.2 us
  Pallas kernels: 52.1 us -> 47.2 us
  other arithmetic: 3.85 us -> 0 us
    pallas_call x1, Pallas kernels: 52.1 us -> 47.2 us  [on_device(): pl.pallas_call(kernel, out_shape=(pltpu.VMEM((1, *shape), F32), pltpu.VME...]
    broadcast_in_dim x1 -> x0, other arithmetic: 3.85 us -> none  [on_device(): return (solution_field[None], residual[None])]
    unnamed x2, local copies, waits for them, and re-layouts: 0.01 us -> 1.41 us
    slice x1 -> x0, local copies, waits for them, and re-layouts: 1.27 us -> none  [on_device(): c0, c1, c2 = (combo[i, 0, 0] for i in range(3))]
where the time goes in v2:
time: 49.4 us; the launch traced here: 49.2 us
  Pallas kernels  47.2 us (96%)
  local copies, waits for them, and re-layouts  1.41 us (3%)
  between operations  0.64 us (1%)
    pallas_call x1, Pallas kernels, on_device(): pl.pallas_call(kernel, out_shape=(pltpu.VMEM((1, *shape), F32), pltpu.VME...  47.2 us
    unnamed x2, local copies, waits for them, and re-layouts  1.41 us

profile of v2, /device:TPU:1, one launch (start us, length us, event | category | flops | bytes accessed | tf_op | source)
XLA Modules:
  0.0 49.2 jit_solution(8951438773254970360)
XLA Ops:
  0.6 47.2 %krylov.1 = (f32[1,2,32,1024]{3,2,1,0:T(8,128)S(1)}, f32[1,2,32,1024]{3,2,1,0:T(8,128)S(1)}) custom-call(f32[2,32,1024]{2,1,0:T(8,128)} %bitcast.6, f32[2,32,1024]{2,1,0:T(8,128)} %bitcast.7, f32[4,2,32,1024]{3,2,1,0:T(8,128)} %bitcast.5, s32[1,32]{1,0:T(1,128)} %block_hbm.1, s32[32,128]{1,0:T(8,128)} %bitcast.8, f32[32,128]{1,0:T(8,128)} %bitcast.9), custom_call_target="tpu_custom_call" | custom-call | tf_op jit(solution)/shard_map/krylov/pallas_call | solution.py:578
  47.8 0.7 %copy.10 = f32[1,2,32,1024]{3,2,1,0:T(8,128)} copy(f32[1,2,32,1024]{3,2,1,0:T(8,128)S(1)} %get-tuple-element.2) | data formatting | bytes 524288
  48.5 0.7 %copy.11 = f32[1,2,32,1024]{3,2,1,0:T(8,128)} copy(f32[1,2,32,1024]{3,2,1,0:T(8,128)S(1)} %get-tuple-element.3) | data formatting | bytes 524288

commit v3 on v2

--- a/solution.py
+++ b/solution.py
@@ -13,9 +13,14 @@
 SCALE = 1.0 / 16.0
 NZ, NYC, NCORE, NT = 8, 8, 2, 4
 NWIN = NZ * NYC * NCORE
+PLANE = NYC * NCORE * NT
 PAIRS = ((0, 0), (0, 1), (1, 1), (0, 2), (1, 2), (2, 2), (0, 3), (1, 3), (2, 3))
 HALO_N, HALO_S, EDGE, STATE, IMAGE, IMAGE_EDGE, ADJ_N, ADJ_S = range(8)
 MESSAGES = 8
+TOWARDS = (0, 1, 2, 2, 3, 3, 0, 1)
+BACK_ROWS = (STEPS + 1) * (LEV * TY + 2 * LEV) * NX // 128
+AHEAD_ROWS = STEPS * (LEV * TY + 2 * LEV) * NX // 128
+SIDE_ROWS = STEPS * 2 * LEV * NX // 128
 ROWS = ((0, 0), (1, TY - 1))
 
 
@@ -123,14 +128,14 @@
     gram_low,
     row_send,
     row_recv,
+    plane_recv,
     local_sem,
     send_sem,
     recv_sem,
-    wsend_sem,
     wrecv_sem,
-    rsend_sem,
     rrecv_sem,
     known_sem,
+    ballast,
 ):
     win = lax.axis_index("win")
     tile = lax.axis_index("tile")
@@ -166,9 +171,10 @@
         start = win + 1 - 2 * core if other_core else win
         return (start + 16 * ((chip_z + by) % NZ - chip_z), tile)
 
-    slot_a = core * NT + tile
+    group = core * NT + tile
+    slot_a = chip_y * 8 + group
     near = [
-        (win - core + ((slot_a + i) % 8) // NT, ((slot_a + i) % 8) % NT) for i in range(1, NCORE * NT)
+        (win - core + ((group + i) % 8) // NT, (group + i) % NT) for i in range(1, NCORE * NT)
     ]
     near += [along_y(1), along_y(-1)]
     near += [along_z(by, other) for by in (1, -1) for other in (False, True)]
@@ -198,8 +204,6 @@
 
     pl.semaphore_wait(barrier, len(near) + jnp.where(has_prev, 1, 0) + jnp.where(has_next, 1, 0))
 
-    started = []
-
     def remote(src, dst, send, recv, peer):
         return pltpu.make_async_remote_copy(
             src_ref=src, dst_ref=dst, send_sem=send, recv_sem=recv, device_id=peer, device_id_type=MESH
@@ -210,8 +214,6 @@
         def _():
             for copy in copies:
                 copy.start()
-
-        started.append((condition, copies))
 
     def wait_if(condition, copies):
         @pl.when(condition)
@@ -230,12 +232,12 @@
             ADJ_N: (adj_edge.at[j, l, 1], adj_n.at[j, l], south_id),
             ADJ_S: (adj_edge.at[j, l, 0], adj_s.at[j, l], north_id),
         }[kind]
-        return remote(src, dst, send_sem.at[j, l, kind], recv_sem.at[j, l, kind], peer)
+        return remote(src, dst, send_sem.at[TOWARDS[kind]], recv_sem.at[j % 2, l, kind], peer)
 
     def weight_messages(l):
         return [
-            remote(weight_edge.at[l], next_weight_edge.at[l], wsend_sem.at[l, 0], wrecv_sem.at[l, 0], prev_id),
-            remote(weight.at[l], next_weight.at[l], wsend_sem.at[l, 1], wrecv_sem.at[l, 1], prev_id),
+            remote(weight_edge.at[l], next_weight_edge.at[l], send_sem.at[2], wrecv_sem.at[l, 0], prev_id),
+            remote(weight.at[l], next_weight.at[l], send_sem.at[2], wrecv_sem.at[l, 1], prev_id),
         ]
 
     row_id = lax.broadcasted_iota(jnp.int32, (8, NX), 0)
@@ -258,8 +260,8 @@
         start_if(has_north, [message(HALO_S, j, l)])
         back = [message(EDGE, j, l), message(STATE, j, l)]
         if j == 0:
-            small, large = weight_messages(l)
-            back = [back[0], small, back[1], large]
+            edges = [x for n in range(LEV) for x in (message(EDGE, 0, n), weight_messages(n)[0])]
+            back = [*(edges if l == 0 else []), back[1], weight_messages(l)[1]]
         start_if(has_prev, back)
         if j == 0 and l == 0:
             loads[2].wait()
@@ -408,9 +410,10 @@
             else:
                 gram(2, l)
         if j + 1 < STEPS:
-            if j == 0:
-                for at in range(2):
-                    pl.semaphore_wait(known_sem.at[at, 1], 2)
+            for at, move in enumerate((along_y, along_z)):
+                pl.semaphore_wait(known_sem.at[at, j + 1], 2)
+                for by in (1, -1) if j == 0 else ():
+                    signal(known_sem.at[at, 2], move(by))
             for l in range(LEV):
                 gram(j, l)
             for l in range(LEV):
@@ -431,64 +434,55 @@
 
     line = packed((total[0][0:1, :], total[1][0:1, :]))
 
-    def received(stage):
-        parts = [row_recv[stage, i] for i in range(8)]
-        return tree2([(x, pltpu.roll(x, 128 - 16, 1)) for x in parts])
-
-    def to_x(i, other):
+    def over_slots(parts):
+        total = tree2([(x, pltpu.roll(x, 128 - 16, 1)) for x in parts])
+        for shift in (4, 2, 1):
+            total = add2(total, rolled(total, shift, 0))
+        return total[0][0:1, :], total[1][0:1, :]
+
+    def arrived(stage, count):
+        whole = ballast.at[pl.ds(0, count)]
+        pltpu.make_async_copy(whole, whole, rrecv_sem.at[stage]).wait()
+
+    def to_plane(by, x_by):
+        where = (along_y(by)[0] - core + 1, (tile + x_by) % NT)
         return remote(
-            row_send.at[0], row_recv.at[0, i], rsend_sem.at[0, other], rrecv_sem.at[0, i], (win - core + 1, other)
+            row_send.at[0], plane_recv.at[pl.ds(slot_a, 1)], send_sem.at[4], rrecv_sem.at[0], where
         )
 
-    def to_y(by):
+    def to_z(by, other_core):
         return remote(
-            row_send.at[1], row_recv.at[1, chip_y], rsend_sem.at[1, by], rrecv_sem.at[1, by], along_y(by)
-        )
-
-    def to_z(by, other_core):
-        at = by + 8 * other_core
-        return remote(
-            row_send.at[2], row_recv.at[2, chip_z], rsend_sem.at[2, at], rrecv_sem.at[2, at], along_z(by, other_core)
+            row_send.at[1], row_recv.at[chip_z], send_sem.at[5], rrecv_sem.at[1], along_z(by, other_core)
         )
 
     is_second = core == 1
     row_send[0] = line
-    for other in range(NT):
-        condition = jnp.logical_or(core == 0, tile != other)
-        start_if(condition, [to_x(slot_a, other)])
+    for by in (4, 3, 5, 2, 6, 1, 7, 0):
+        for other in (2, 1, 3, 0):
+            copy = to_plane(by, other)
+            if by == 0 and other == 0:
+                pl.when(core == 0)(copy.start)
+            else:
+                copy.start()
 
     @pl.when(is_second)
     def _():
-        row_recv[0, slot_a] = line
-        for i in range(NCORE * NT):
-
-            @pl.when(slot_a != i)
-            def _(i=i):
-                to_x(i, 0).wait_recv()
-
-        mine = packed(received(0))
+        plane_recv[pl.ds(slot_a, 1), :] = line
+        arrived(0, PLANE - 1)
+        mine = packed(over_slots([plane_recv[8 * i : 8 * i + 8, :] for i in range(PLANE // 8)]))
         row_send[1] = mine
-        row_recv[1, chip_y] = mine
-        for by in range(1, NYC):
-            to_y(by).start()
-        for by in range(1, NYC):
-            to_y(by).wait_recv()
-        mine = packed(received(1))
-        row_send[2] = mine
-        row_recv[2, chip_z] = mine
+        row_recv[chip_z] = mine
         for by in range(1, NZ):
             to_z(by, True).start()
             to_z(by, False).start()
         to_z(0, True).start()
-        for by in range(1, NZ):
-            to_z(by, False).wait_recv()
+        arrived(1, NZ - 1)
 
     @pl.when(jnp.logical_not(is_second))
     def _():
-        for by in range(NZ):
-            to_z(by, True).wait_recv()
-
-    total = received(2)
+        arrived(1, NZ)
+
+    total = tree2([(x, pltpu.roll(x, 128 - 16, 1)) for x in [row_recv[i] for i in range(NZ)]])
     line = packed(total)
 
     def value(i, j):
@@ -512,21 +506,19 @@
             solution_out[0, l, rows(b), :] = SCALE * (combo[0] * u0 + combo[1] * u1 + combo[2] * u2)
             residual_out[0, l, rows(b), :] = u0 - combo[0] * u1 - combo[1] * u2 - combo[2] * u3
 
-    for condition, copies in started:
-
+    def sent(condition, count, semaphore):
         @pl.when(condition)
-        def _(copies=copies):
-            for copy in copies:
-                copy.wait_send()
-
-    @pl.when(is_second)
-    def _():
-        for by in range(1, NYC):
-            to_y(by).wait_send()
-        for by in range(1, NZ):
-            to_z(by, True).wait_send()
-            to_z(by, False).wait_send()
-        to_z(0, True).wait_send()
+        def _():
+            whole = ballast.at[pl.ds(0, count)]
+            pltpu.make_async_copy(whole, whole, semaphore).wait()
+
+    sent(has_south, SIDE_ROWS, send_sem.at[0])
+    sent(has_north, SIDE_ROWS, send_sem.at[1])
+    sent(has_prev, BACK_ROWS, send_sem.at[2])
+    sent(has_next, AHEAD_ROWS, send_sem.at[3])
+    sent(is_second, PLANE // 2 - 1, send_sem.at[4])
+    sent(jnp.logical_not(is_second), PLANE // 2, send_sem.at[4])
+    sent(is_second, 2 * NZ - 1, send_sem.at[5])
 
 
 def on_device(right_side, error_weight, coeffs, obs_block, obs_pos, obs_weight):
@@ -564,18 +556,18 @@
         vmem(shape, F32),
         vmem((len(PAIRS), 8, 128), F32),
         vmem((len(PAIRS), 8, 128), F32),
-        vmem((3, 1, 128), F32),
-        vmem((3, 8, 1, 128), F32),
+        vmem((2, 1, 128), F32),
+        vmem((NZ, 1, 128), F32),
+        vmem((PLANE, 128), F32),
         pltpu.SemaphoreType.DMA((6,)),
-        pltpu.SemaphoreType.DMA((STEPS, LEV, MESSAGES)),
-        pltpu.SemaphoreType.DMA((STEPS, LEV, MESSAGES)),
+        pltpu.SemaphoreType.DMA((6,)),
+        pltpu.SemaphoreType.DMA((2, LEV, MESSAGES)),
         pltpu.SemaphoreType.DMA((LEV, 2)),
-        pltpu.SemaphoreType.DMA((LEV, 2)),
-        pltpu.SemaphoreType.DMA((3, 16)),
-        pltpu.SemaphoreType.DMA((3, 16)),
-        pltpu.SemaphoreType.REGULAR((2, 2)),
+        pltpu.SemaphoreType.DMA((2,)),
+        pltpu.SemaphoreType.REGULAR((2, 3)),
+        vmem((BACK_ROWS, 1, 128), F32),
     ]
-    return pl.pallas_call(
+    solution_field, residual = pl.pallas_call(
         kernel,
         out_shape=(pltpu.VMEM((1, *shape), F32), pltpu.VMEM((1, *shape), F32)),
         in_specs=[pl.BlockSpec(memory_space=hbm)] * 6,
@@ -591,6 +583,26 @@
         obs_pos.reshape(32, 128),
         obs_weight.reshape(32, 128),
     )
+    whole = jax.ShapeDtypeStruct((1, *shape), F32)
+    return pl.pallas_call(
+        store,
+        out_shape=(whole, whole),
+        in_specs=[pl.BlockSpec(memory_space=vmem)] * 2,
+        out_specs=(pl.BlockSpec(memory_space=hbm),) * 2,
+        scratch_shapes=[pltpu.SemaphoreType.DMA((2,))],
+        name="store",
+    )(*(pltpu.with_memory_space_constraint(x, vmem) for x in (solution_field, residual)))
+
+
+def store(solution_field, residual, solution_out, residual_out, sem):
+    copies = [
+        pltpu.make_async_copy(solution_field, solution_out, sem.at[0]),
+        pltpu.make_async_copy(residual, residual_out, sem.at[1]),
+    ]
+    for copy in copies:
+        copy.start()
+    for copy in copies:
+        copy.wait()
 
 
 def solution(mesh):

time: 49.4 us -> 46.2 us (0.935)
  Pallas kernels: 47.2 us -> 45.5 us
  local copies, waits for them, and re-layouts: 1.41 us -> 0 us
    pallas_call x1, Pallas kernels: 47.2 us -> 44.7 us  [on_device(): pl.pallas_call(kernel, out_shape=(pltpu.VMEM((1, *shape), F32), pltpu.VME...]
    unnamed x2 -> x0, local copies, waits for them, and re-layouts: 1.41 us -> none
    pallas_call x0 -> x1, Pallas kernels: none -> 0.81 us  [on_device(): pl.pallas_call(store, out_shape=(whole, whole), in_specs=[pl.BlockSpec(me...]
where the time goes in v3:
time: 46.2 us; the launch traced here: 46.1 us
  Pallas kernels  45.5 us (98%)
  between operations  0.64 us (1%)
    pallas_call x1, Pallas kernels, on_device(): pl.pallas_call(kernel, out_shape=(pltpu.VMEM((1, *shape), F32), pltpu.VME...  44.7 us

profile of v3, /device:TPU:1, one launch (start us, length us, event | category | flops | bytes accessed | tf_op | source)
XLA Modules:
  0.0 46.1 jit_solution(14501640306461079878)
XLA Ops:
  0.6 44.7 %krylov.1 = (f32[1,2,32,1024]{3,2,1,0:T(8,128)S(1)}, f32[1,2,32,1024]{3,2,1,0:T(8,128)S(1)}) custom-call(f32[2,32,1024]{2,1,0:T(8,128)} %bitcast.6, f32[2,32,1024]{2,1,0:T(8,128)} %bitcast.7, f32[4,2,32,1024]{3,2,1,0:T(8,128)} %bitcast.5, s32[1,32]{1,0:T(1,128)} %block_hbm.1, s32[32,128]{1,0:T(8,128)} %bitcast.8, f32[32,128]{1,0:T(8,128)} %bitcast.9), custom_call_target="tpu_custom_call" | custom-call | tf_op jit(solution)/shard_map/krylov/pallas_call | solution.py:570
  45.3 0.8 %store.1 = (f32[1,2,32,1024]{3,2,1,0:T(8,128)}, f32[1,2,32,1024]{3,2,1,0:T(8,128)}) custom-call(f32[1,2,32,1024]{3,2,1,0:T(8,128)S(1)} %get-tuple-element.4.solution_field, f32[1,2,32,1024]{3,2,1,0:T(8,128)S(1)} %get-tuple-element.5.residual), custom_call_target="tpu_custom_call" | custom-call | tf_op jit(solution)/shard_map/store/pallas_call | solution.py:587

commit v4 on v3

v4 whole, which is shorter than its diff:
```python
import jax
import jax.numpy as jnp
from jax import lax
from jax.experimental import pallas as pl
from jax.experimental.pallas import tpu as pltpu
from jax.sharding import PartitionSpec as P

MESH = pl.DeviceIdType.MESH
F32 = jnp.float32
LEV, TY, NX = 2, 32, 1024
BLOCKS = TY // 8
STEPS = 3
SCALE = 1.0 / 16.0
NZ, NYC, NCORE, NT = 8, 8, 2, 4
NWIN = NZ * NYC * NCORE
PLANE = NYC * NCORE * NT
PAIRS = ((0, 0), (0, 1), (1, 1), (0, 2), (1, 2), (2, 2), (0, 3), (1, 3), (2, 3))
HALO, BACK, FORE, STATE, IMAGE = 0, 2, 4, 6, 10
MESSAGES = 14
WIDE = NX // 128
SIDE_ROWS = LEV * (2 * STEPS + 4) * WIDE
BACK_ROWS = (STEPS + 1) * LEV * TY * WIDE
AHEAD_ROWS = (STEPS * LEV * TY + 2 * LEV) * WIDE
BACK_SIDE_ROWS = LEV * (STEPS + 1) * WIDE
AHEAD_SIDE_ROWS = LEV * STEPS * WIDE
EARLY = 6
OUTER = ((0, 1), (TY - 1, TY - 2))


def two_sum(a, b):
    s = a + b
    t = s - a
    return s, (a - (s - t)) + (b - t)


def quick_sum(a, b):
    s = a + b
    return s, b - (s - a)


def split(a):
    c = a * 4097.0
    high = c - (c - a)
    return high, a - high


def two_prod_split(a, b, sa, sb):
    p = a * b
    return p, ((sa[0] * sb[0] - p) + sa[0] * sb[1] + sa[1] * sb[0]) + sa[1] * sb[1]


def two_prod(a, b):
    return two_prod_split(a, b, split(a), split(b))


def add2(a, b):
    s, e = two_sum(a[0], b[0])
    return quick_sum(s, e + (a[1] + b[1]))


def neg2(a):
    return -a[0], -a[1]


def sub2(a, b):
    return add2(a, neg2(b))


def mul2(a, b):
    p, e = two_prod(a[0], b[0])
    return quick_sum(p, e + (a[0] * b[1] + a[1] * b[0]))


def div2(a, b):
    zero = jnp.zeros_like(a[0])
    first = a[0] / b[0]
    rest = sub2(a, mul2((first, zero), b))
    return quick_sum(first, rest[0] / b[0])


def plus(a, b):
    s, e = two_sum(a[0], b[0])
    return s, (a[1] + b[1]) + e


def tree2(items):
    while len(items) > 1:
        items = [
            plus(items[i], items[i + 1]) if i + 1 < len(items) else items[i]
            for i in range(0, len(items), 2)
        ]
    return items[0]


def rolled(pair, shift, axis):
    return pltpu.roll(pair[0], shift, axis), pltpu.roll(pair[1], shift, axis)


def kernel(
    right_hbm,
    weight_hbm,
    coeff_hbm,
    block_hbm,
    pos_hbm,
    obsw_hbm,
    solution_out,
    residual_out,
    v0,
    v1,
    v2,
    v3,
    weight,
    coeff,
    block,
    pos,
    obsw,
    diag,
    edge,
    coeff_edge,
    centre_edge,
    weight_edge,
    halo,
    coeff_halo,
    weight_halo,
    next_halo,
    prev_halo,
    prev_centre,
    next_state,
    next_weight,
    image,
    before,
    spread_halo,
    follow,
    spread,
    gram_high,
    gram_low,
    gram_line,
    row_send,
    row_recv,
    plane_recv,
    local_sem,
    send_sem,
    recv_sem,
    once_sem,
    rrecv_sem,
    known_sem,
    ballast,
):
    win = lax.axis_index("win")
    tile = lax.axis_index("tile")
    core = win % 2
    chip_y = (win // 2) % 8
    chip_z = win // 16
    has_prev, has_next = win > 0, win < NWIN - 1
    has_north, has_south = tile > 0, tile < NT - 1
    prev_id, next_id = (win - 1, tile), (win + 1, tile)
    states = (v0, v1, v2, v3)

    loads = [
        pltpu.make_async_copy(src, dst, local_sem.at[i])
        for i, (src, dst) in enumerate(
            (
                (right_hbm, v0),
                (weight_hbm, weight),
                (coeff_hbm, coeff),
                (block_hbm, block),
                (pos_hbm, pos),
                (obsw_hbm, obsw),
            )
        )
    ]
    for load in loads:
        load.start()

    def along_y(by):
        return (win + 2 * ((chip_y + by) % NYC - chip_y), tile)

    def along_z(by, other_core=False):
        start = win + 1 - 2 * core if other_core else win
        return (start + 16 * ((chip_z + by) % NZ - chip_z), tile)

    group = core * NT + tile
    slot_a = chip_y * 8 + group
    near = [
        (win - core + ((group + i) % 8) // NT, (group + i) % NT) for i in range(1, NCORE * NT)
    ]
    near += [along_y(1), along_y(-1)]
    near += [along_z(by, other) for by in (1, -1) for other in (False, True)]

    def signal(semaphore, peer):
        pl.semaphore_signal(semaphore, inc=1, device_id=peer, device_id_type=MESH)

    barrier = pltpu.get_barrier_semaphore()

    @pl.when(has_prev)
    def _():
        signal(barrier, prev_id)

    @pl.when(has_next)
    def _():
        signal(barrier, next_id)

    for peer in near:
        signal(barrier, peer)

    for i in range(2):
        loads[i].wait()
    for side in range(2):
        for l in range(LEV):
            for n, row in enumerate(OUTER[side]):
                edge[0, l, side, n] = v0[l, row : row + 1, :]
            row = OUTER[side][0]
            weight_edge[side, l] = weight[l, row : row + 1, :]

    pl.semaphore_wait(barrier, len(near) + jnp.where(has_prev, 1, 0) + jnp.where(has_next, 1, 0))

    def remote(src, dst, send, recv, peer):
        return pltpu.make_async_remote_copy(
            src_ref=src, dst_ref=dst, send_sem=send, recv_sem=recv, device_id=peer, device_id_type=MESH
        )

    def start_if(condition, copies):
        @pl.when(condition)
        def _():
            for copy in copies:
                copy.start()

    def wait_if(condition, copies):
        @pl.when(condition)
        def _():
            for copy in copies:
                copy.wait_recv()

    beside = (has_north, has_south)

    def towards(side, by):
        return (win + by, tile + (1 if side else -1))

    def and_(*conditions):
        total = conditions[0]
        for condition in conditions[1:]:
            total = jnp.logical_and(total, condition)
        return total

    def to_side(kind, j, l, side):
        sem = recv_sem.at[j % 2, l, kind + 1 - side]
        if kind == HALO:
            return remote(edge.at[j, l, side], halo.at[j, l, 1 - side], send_sem.at[side], sem, towards(side, 0))
        dst, out, by = (next_halo, 4, -1) if kind == BACK else (prev_halo, 6, 1)
        return remote(
            edge.at[j, l, side, 0], dst.at[j, l, 1 - side], send_sem.at[out + side], sem, towards(side, by)
        )

    def send_edges(j, l, side, diagonal=True, straight=True):
        if straight:
            start_if(beside[side], [to_side(HALO, j, l, side)])
        if diagonal:
            start_if(and_(beside[side], has_prev), [to_side(BACK, j, l, side)])
            start_if(and_(beside[side], has_next), [to_side(FORE, j, l, side)])

    def edges_from(kind, j, l, side):
        extra = {HALO: (), BACK: (has_next,), FORE: (has_prev,)}[kind]
        wait_if(and_(beside[side], *extra), [to_side(kind, j, l, 1 - side)])

    def state_block(j, l, b):
        at = pl.ds(8 * b, 8)
        return remote(
            states[j].at[l, at], next_state.at[j, l, at], send_sem.at[2], recv_sem.at[j % 2, l, STATE + b], prev_id
        )

    def image_block(j, l, b):
        at = pl.ds(8 * b, 8)
        return remote(
            image.at[j, l, at], before.at[j, l, at], send_sem.at[3], recv_sem.at[j % 2, l, IMAGE + b], next_id
        )

    def first_block(l, b):
        return state_block(0, l, b)

    def weight_block(l, b):
        at = pl.ds(8 * b, 8)
        return remote(
            weight.at[l, at], next_weight.at[l, at], send_sem.at[2], once_sem.at[5 + BLOCKS * l + b], prev_id
        )

    def coeff_side(side):
        return remote(
            coeff_edge.at[side], coeff_halo.at[1 - side], send_sem.at[side], once_sem.at[1 - side], towards(side, 0)
        )

    def weight_side(side):
        return remote(
            weight_edge.at[side],
            weight_halo.at[1 - side],
            send_sem.at[4 + side],
            once_sem.at[3 - side],
            towards(side, -1),
        )

    def centre_ahead():
        return remote(centre_edge, prev_centre, send_sem.at[3], once_sem.at[4], next_id)

    row_id = lax.broadcasted_iota(jnp.int32, (8, NX), 0)
    first_row, last_row = row_id == 0, row_id == 7

    def rows(b):
        return slice(8 * b, 8 * b + 8)

    def vertical(ref, l, b, top=0.0, bottom=0.0):
        here = ref[l, rows(b), :]
        above = pltpu.roll(ref[l, rows(b - 1), :], 1, 0) if b > 0 else top
        below = pltpu.roll(ref[l, rows(b + 1), :], 7, 0) if b < BLOCKS - 1 else bottom
        north = jnp.where(first_row, above, pltpu.roll(here, 1, 0))
        south = jnp.where(last_row, below, pltpu.roll(here, 7, 0))
        return north + south

    def edge_only(side, value):
        return jnp.where((first_row, last_row)[side], value, 0.0)

    def propagate(j, l, b):
        v = states[j]
        here = v[l, rows(b), :]
        image[j, l, rows(b), :] = (
            coeff[0, l, rows(b), :] * here
            + coeff[1, l, rows(b), :] * vertical(v, l, b)
            + coeff[2, l, rows(b), :] * pltpu.roll(here, NX - 1, 1)
            + coeff[3, l, rows(b), :] * pltpu.roll(here, 1, 1)
        )
        if j > 0 or l == 0:
            start_if(has_next, [image_block(j, l, b)])

    def side_of(b):
        return {0: 0, BLOCKS - 1: 1}.get(b)

    def outside(j, l, side):
        edges_from(HALO, j, l, side)
        if j == 0 and l == 0:
            wait_if(beside[side], [coeff_side(1 - side)])
            wait_if(and_(beside[side], has_next), [weight_side(1 - side)])
        near_row, far_row = halo[j, l, side, 0], halo[j, l, side, 1]
        row = OUTER[side][0]
        here = (
            coeff_halo[side, l, 0] * near_row
            + coeff_halo[side, l, 1] * (far_row + states[j][l, row : row + 1, :])
            + coeff_halo[side, l, 2] * pltpu.roll(near_row, NX - 1, 1)
            + coeff_halo[side, l, 3] * pltpu.roll(near_row, 1, 1)
        )
        edges_from(BACK, j, l, side)
        f = weight_halo[side, l] * (next_halo[j, l, side] - here)
        spread_halo[l, side] = coeff_halo[side, l, 1] * f

    def finish(j, l, b):
        v, out = states[j], states[j + 1]
        side = side_of(b)
        f = follow[l, rows(b), :]
        top = spread_halo[l, 0] if side == 0 else 0.0
        bottom = spread_halo[l, 1] if side == 1 else 0.0
        back_image = (
            coeff[0, l, rows(b), :] * f
            + vertical(spread, l, b, top, bottom)
            + pltpu.roll(coeff[2, l, rows(b), :] * f, 1, 1)
            + pltpu.roll(coeff[3, l, rows(b), :] * f, NX - 1, 1)
        )
        here = v[l, rows(b), :]
        out[l, rows(b), :] = weight[l, rows(b), :] * here - back_image + diag[l, rows(b), :] * here
        wait_if(has_prev, [image_block(j, l, b)])
        came = before[j, l, rows(b), :]
        if side is not None:
            edges_from(FORE, j, l, side)
            if j == 0 and l == 0 and side == 0:
                wait_if(has_prev, [centre_ahead()])
            came = came + edge_only(side, prev_centre[l, side] * prev_halo[j, l, side])
        out[l, rows(b), :] = SCALE * (out[l, rows(b), :] - weight[l, rows(b), :] * came)
        if j + 1 == STEPS:
            return
        start_if(has_prev, [state_block(j + 1, l, b)])
        if side is not None:
            for n, row in enumerate(OUTER[side]):
                edge[j + 1, l, side, n] = out[l, row : row + 1, :]
            send_edges(j + 1, l, side)
        if b > 0:
            propagate(j + 1, l, b - 1)
        if b == BLOCKS - 1:
            propagate(j + 1, l, b)

    def complete(j, l):
        for b in range(BLOCKS):
            side = side_of(b)
            if side is not None:
                outside(j, l, side)
            wait_if(has_next, [state_block(j, l, b), *([weight_block(l, b)] if j == 0 else [])])
            sent_image = image[j, l, rows(b), :]
            if side is not None:
                sent_image = sent_image + edge_only(side, coeff[1, l, rows(b), :] * halo[j, l, side, 0])
            f = next_weight[l, rows(b), :] * (next_state[j, l, rows(b), :] - sent_image)
            follow[l, rows(b), :] = f
            spread[l, rows(b), :] = coeff[1, l, rows(b), :] * f
            if b > 0:
                finish(j, l, b - 1)
        finish(j, l, BLOCKS - 1)

    def gram(group, l):
        indices = range(3 * group, 3 * group + 3)
        zero = jnp.zeros((8, 128), F32)

        def step(b, acc):
            acc = list(acc)
            at = pl.ds(pl.multiple_of(b * 8, 8), 8)
            for c in range(NX // 128):
                parts = {}
                for index in indices:
                    for s in PAIRS[index]:
                        if s not in parts:
                            x = states[s][l, at, c * 128 : (c + 1) * 128]
                            parts[s] = (x, split(x))
                for n, index in enumerate(indices):
                    i, k = PAIRS[index]
                    p, e = two_prod_split(parts[i][0], parts[k][0], parts[i][1], parts[k][1])
                    s, f = two_sum(acc[2 * n], p)
                    acc[2 * n], acc[2 * n + 1] = s, acc[2 * n + 1] + (e + f)
            return tuple(acc)

        acc = lax.fori_loop(0, BLOCKS, step, (zero,) * 6)
        for n, index in enumerate(indices):
            part = (acc[2 * n], acc[2 * n + 1])
            if l == 0:
                gram_high[index], gram_low[index] = part
                continue
            part = over_rows(plus(part, (gram_high[index], gram_low[index])))
            gram_line[index : index + 1, :], gram_line[16 + index : 17 + index, :] = part

    def over_rows(total):
        for shift in (4, 2, 1):
            total = plus(total, rolled(total, shift, 0))
        return total[0][0:1, :], total[1][0:1, :]

    def observed_weights():
        pos_t = jnp.swapaxes(pos[...], 0, 1)
        obsw_t = jnp.swapaxes(obsw[...], 0, 1)
        lane = lax.broadcasted_iota(jnp.int32, (128, 128), 1)
        lines = []
        for b in range(32):
            hit = pos_t[:, b : b + 1] == lane
            lines.append(jnp.sum(jnp.where(hit, obsw_t[:, b : b + 1], 0.0), axis=0, keepdims=True))
        per_block = jnp.concatenate(lines, axis=0)
        row = lax.broadcasted_iota(jnp.int32, (LEV * TY, 32), 0)
        for c in range(NX // 128):
            hot = (block[...] == row * (NX // 128) + c).astype(F32)
            out = jnp.dot(hot, per_block, precision=lax.Precision.HIGHEST, preferred_element_type=F32)
            for l in range(LEV):
                diag[l, :, c * 128 : (c + 1) * 128] = out[l * TY : (l + 1) * TY, :]

    def zeros(*refs):
        for ref in refs:
            ref[...] = jnp.zeros(ref.shape, F32)

    gram_line[...] = jnp.zeros((128, 128), F32)
    for side in range(2):
        for by in range(LEV):
            send_edges(0, by, side, diagonal=False)
        pl.when(beside[side])(lambda side=side: signal(known_sem.at[2, 0], towards(side, 0)))
    blocks = [copy(l, b) for l in range(LEV) for b in range(BLOCKS) for copy in (first_block, weight_block)]
    start_if(has_prev, blocks[:EARLY])
    loads[2].wait()
    for l in range(LEV):
        for b in range(BLOCKS):
            propagate(0, l, b)
    for at, move in enumerate((along_y, along_z)):
        for by in (1, -1):
            signal(known_sem.at[at, 0], move(by))
    pl.semaphore_wait(known_sem.at[2, 0], jnp.where(has_north, 1, 0) + jnp.where(has_south, 1, 0))
    for side in range(2):
        start_if(and_(beside[side], has_prev), [weight_side(side)])
        for l in range(LEV):
            send_edges(0, l, side, straight=False)
    start_if(has_prev, blocks[EARLY:])
    for side in range(2):
        row = OUTER[side][0]
        for l in range(LEV):
            for n in range(4):
                coeff_edge[side, l, n] = coeff[n, l, row : row + 1, :]
            centre_edge[l, side] = coeff[1, l, row : row + 1, :]
    for side in range(2):
        start_if(beside[side], [coeff_side(side)])
    start_if(has_next, [centre_ahead()])
    start_if(has_next, [image_block(0, 1, b) for b in range(BLOCKS)])
    for side in range(2):

        @pl.when(jnp.logical_not(beside[side]))
        def _(side=side):
            zeros(coeff_halo.at[side], weight_halo.at[side])
            for j in range(STEPS):
                for l in range(LEV):
                    zeros(halo.at[j, l, side], next_halo.at[j, l, side], prev_halo.at[j, l, side])

    pl.when(jnp.logical_not(has_prev))(lambda: zeros(before, prev_halo, prev_centre))
    pl.when(jnp.logical_not(has_next))(lambda: zeros(next_state, next_weight, next_halo, weight_halo))
    for load in loads[3:]:
        load.wait()
    observed_weights()
    for at, move in enumerate((along_y, along_z)):
        pl.semaphore_wait(known_sem.at[at, 0], 2)
        for by in (2, -2):
            signal(known_sem.at[at, 1], move(by))
    for j in range(STEPS):
        for l in range(LEV):
            complete(j, l)
            if j + 1 == STEPS:
                gram(2, l)
        if j + 1 < STEPS:
            for at, move in enumerate((along_y, along_z)):
                pl.semaphore_wait(known_sem.at[at, j + 1], 2)
                for by in (1, -1) if j == 0 else ():
                    signal(known_sem.at[at, 2], move(by))
            for l in range(LEV):
                gram(j, l)

    turned = jnp.swapaxes(gram_line[...], 0, 1)
    pieces = [turned[8 * i : 8 * i + 8, :] for i in range(16)]
    total = over_rows(tree2([(x, pltpu.roll(x, 128 - 16, 1)) for x in pieces]))
    lane = lax.broadcasted_iota(jnp.int32, (1, 128), 1)

    def packed(pair):
        return jnp.where(lane < 16, pair[0], jnp.where(lane < 32, pltpu.roll(pair[1], 16, 1), 0.0))

    line = packed(total)

    def over_slots(parts):
        return over_rows(tree2([(x, pltpu.roll(x, 128 - 16, 1)) for x in parts]))

    def arrived(stage, count):
        whole = ballast.at[pl.ds(0, count)]
        pltpu.make_async_copy(whole, whole, rrecv_sem.at[stage]).wait()

    def to_plane(by, x_by):
        where = (along_y(by)[0] - core + 1, (tile + x_by) % NT)
        return remote(
            row_send.at[0], plane_recv.at[pl.ds(slot_a, 1)], send_sem.at[8], rrecv_sem.at[0], where
        )

    def to_z(by, other_core):
        return remote(
            row_send.at[1], row_recv.at[chip_z], send_sem.at[9], rrecv_sem.at[1], along_z(by, other_core)
        )

    is_second = core == 1
    row_send[0] = line
    for by in (4, 3, 5, 2, 6, 1, 7, 0):
        for other in (2, 1, 3, 0):
            copy = to_plane(by, other)
            if by == 0 and other == 0:
                pl.when(core == 0)(copy.start)
            else:
                copy.start()

    @pl.when(is_second)
    def _():
        plane_recv[pl.ds(slot_a, 1), :] = line
        arrived(0, PLANE - 1)
        mine = packed(over_slots([plane_recv[8 * i : 8 * i + 8, :] for i in range(PLANE // 8)]))
        row_send[1] = mine
        row_recv[chip_z] = mine
        for by in (4, 3, 5, 2, 6, 1, 7):
            to_z(by, True).start()
            to_z(by, False).start()
        to_z(0, True).start()
        arrived(1, NZ - 1)

    @pl.when(jnp.logical_not(is_second))
    def _():
        arrived(1, NZ)

    total = tree2([(x, pltpu.roll(x, 128 - 16, 1)) for x in [row_recv[i] for i in range(NZ)]])
    line = packed(quick_sum(*total))

    def value(i, j):
        at = PAIRS.index((min(i, j), max(i, j)))
        return tuple(jnp.broadcast_to(line[:, at + off : at + off + 1], (8, 128)) for off in (0, 16))

    a = [[value(i, n + 1) for n in range(3)] + [value(i, 0)] for i in range(3)]
    for pivot in range(2):
        for i in range(pivot + 1, 3):
            factor = div2(a[i][pivot], a[pivot][pivot])
            for n in range(pivot + 1, 4):
                a[i][n] = sub2(a[i][n], mul2(factor, a[pivot][n]))
    c2 = div2(a[2][3], a[2][2])
    c1 = div2(sub2(a[1][3], mul2(a[1][2], c2)), a[1][1])
    c0 = div2(sub2(sub2(a[0][3], mul2(a[0][1], c1)), mul2(a[0][2], c2)), a[0][0])
    combo = [jnp.concatenate([c[0]] * (NX // 128), axis=1) for c in (c0, c1, c2)]
    for l in range(LEV):
        for b in range(BLOCKS):
            at = (l, rows(b), slice(None))
            u0, u1, u2, u3 = (s[at] for s in states)
            solution_out[0, l, rows(b), :] = SCALE * (combo[0] * u0 + combo[1] * u1 + combo[2] * u2)
            residual_out[0, l, rows(b), :] = u0 - combo[0] * u1 - combo[1] * u2 - combo[2] * u3

    def sent(condition, count, semaphore):
        @pl.when(condition)
        def _():
            whole = ballast.at[pl.ds(0, count)]
            pltpu.make_async_copy(whole, whole, semaphore).wait()

    for side in range(2):
        sent(beside[side], SIDE_ROWS, send_sem.at[side])
        sent(and_(beside[side], has_prev), BACK_SIDE_ROWS, send_sem.at[4 + side])
        sent(and_(beside[side], has_next), AHEAD_SIDE_ROWS, send_sem.at[6 + side])
    sent(has_prev, BACK_ROWS, send_sem.at[2])
    sent(has_next, AHEAD_ROWS, send_sem.at[3])
    sent(is_second, PLANE // 2 - 1, send_sem.at[8])
    sent(jnp.logical_not(is_second), PLANE // 2, send_sem.at[8])
    sent(is_second, 2 * NZ - 1, send_sem.at[9])


def on_device(right_side, error_weight, coeffs, obs_block, obs_pos, obs_weight):
    shape = (LEV, TY, NX)
    vmem, hbm = pltpu.VMEM, pltpu.HBM
    line = (STEPS, LEV, 2, 1, NX)
    scratch = [
        vmem(shape, F32),
        vmem(shape, F32),
        vmem(shape, F32),
        vmem(shape, F32),
        vmem(shape, F32),
        vmem((4, *shape), F32),
        vmem((1, 32), jnp.int32),
        vmem((32, 128), jnp.int32),
        vmem((32, 128), F32),
        vmem(shape, F32),
        vmem((STEPS, LEV, 2, 2, 1, NX), F32),
        vmem((2, LEV, 4, 1, NX), F32),
        vmem((LEV, 2, 1, NX), F32),
        vmem((2, LEV, 1, NX), F32),
        vmem((STEPS, LEV, 2, 2, 1, NX), F32),
        vmem((2, LEV, 4, 1, NX), F32),
        vmem((2, LEV, 1, NX), F32),
        vmem(line, F32),
        vmem(line, F32),
        vmem((LEV, 2, 1, NX), F32),
        vmem((STEPS, *shape), F32),
        vmem(shape, F32),
        vmem((STEPS, *shape), F32),
        vmem((STEPS, *shape), F32),
        vmem((LEV, 2, 1, NX), F32),
        vmem(shape, F32),
        vmem(shape, F32),
        vmem((len(PAIRS), 8, 128), F32),
        vmem((len(PAIRS), 8, 128), F32),
        vmem((128, 128), F32),
        vmem((2, 1, 128), F32),
        vmem((NZ, 1, 128), F32),
        vmem((PLANE, 128), F32),
        pltpu.SemaphoreType.DMA((6,)),
        pltpu.SemaphoreType.DMA((10,)),
        pltpu.SemaphoreType.DMA((2, LEV, MESSAGES)),
        pltpu.SemaphoreType.DMA((5 + LEV * BLOCKS,)),
        pltpu.SemaphoreType.DMA((2,)),
        pltpu.SemaphoreType.REGULAR((3, 3)),
        vmem((BACK_ROWS, 1, 128), F32),
    ]
    solution_field, residual = pl.pallas_call(
        kernel,
        out_shape=(pltpu.VMEM((1, *shape), F32), pltpu.VMEM((1, *shape), F32)),
        in_specs=[pl.BlockSpec(memory_space=hbm)] * 6,
        out_specs=(pl.BlockSpec(memory_space=vmem),) * 2,
        scratch_shapes=scratch,
        compiler_params=pltpu.CompilerParams(collective_id=0, has_side_effects=True),
        name="krylov",
    )(
        right_side.reshape(shape),
        error_weight.reshape(shape),
        coeffs.reshape(4, *shape),
        obs_block,
        obs_pos.reshape(32, 128),
        obs_weight.reshape(32, 128),
    )
    whole = jax.ShapeDtypeStruct((1, *shape), F32)
    return pl.pallas_call(
        store,
        out_shape=(whole, whole),
        in_specs=[pl.BlockSpec(memory_space=vmem)] * 2,
        out_specs=(pl.BlockSpec(memory_space=hbm),) * 2,
        scratch_shapes=[pltpu.SemaphoreType.DMA((2,))],
        name="store",
    )(*(pltpu.with_memory_space_constraint(x, vmem) for x in (solution_field, residual)))


def store(solution_field, residual, solution_out, residual_out, sem):
    copies = [
        pltpu.make_async_copy(solution_field, solution_out, sem.at[0]),
        pltpu.make_async_copy(residual, residual_out, sem.at[1]),
    ]
    for copy in copies:
        copy.start()
    for copy in copies:
        copy.wait()


def solution(mesh):
    in_specs = (
        P("win", None, "tile", None),
        P("win", None, "tile", None),
        P(None, "win", None, "tile", None),
        P("win", "tile"),
        P("win", "tile", None),
        P("win", "tile", None),
    )
    out_specs = (P("win", None, "tile", None), P("win", None, "tile", None))
    return jax.shard_map(on_device, mesh=mesh, in_specs=in_specs, out_specs=out_specs, check_vma=False)
```

time: 46.2 us -> 43.7 us (0.946)
  Pallas kernels: 45.5 us -> 42.9 us
    pallas_call x1, Pallas kernels: 44.7 us -> 42.1 us  [on_device(): pl.pallas_call(kernel, out_shape=(pltpu.VMEM((1, *shape), F32), pltpu.VME...]
where the time goes in v4:
time: 43.7 us; the launch traced here: 43.6 us
  Pallas kernels  42.9 us (98%)
  between operations  0.64 us (1%)
    pallas_call x1, Pallas kernels, on_device(): pl.pallas_call(kernel, out_shape=(pltpu.VMEM((1, *shape), F32), pltpu.VME...  42.1 us

profile of v4, /device:TPU:1, one launch (start us, length us, event | category | flops | bytes accessed | tf_op | source)
XLA Modules:
  0.0 43.6 jit_solution(2134450022737145816)
XLA Ops:
  0.6 42.1 %krylov.1 = (f32[1,2,32,1024]{3,2,1,0:T(8,128)S(1)}, f32[1,2,32,1024]{3,2,1,0:T(8,128)S(1)}) custom-call(f32[2,32,1024]{2,1,0:T(8,128)} %bitcast.6, f32[2,32,1024]{2,1,0:T(8,128)} %bitcast.7, f32[4,2,32,1024]{3,2,1,0:T(8,128)} %bitcast.5, s32[1,32]{1,0:T(1,128)} %block_hbm.1, s32[32,128]{1,0:T(8,128)} %bitcast.8, f32[32,128]{1,0:T(8,128)} %bitcast.9), custom_call_target="tpu_custom_call" | custom-call | tf_op jit(solution)/shard_map/krylov/pallas_call | solution.py:660
  42.7 0.8 %store.1 = (f32[1,2,32,1024]{3,2,1,0:T(8,128)}, f32[1,2,32,1024]{3,2,1,0:T(8,128)}) custom-call(f32[1,2,32,1024]{3,2,1,0:T(8,128)S(1)} %get-tuple-element.4.solution_field, f32[1,2,32,1024]{3,2,1,0:T(8,128)S(1)} %get-tuple-element.5.residual), custom_call_target="tpu_custom_call" | custom-call | tf_op jit(solution)/shard_map/store/pallas_call | solution.py:677

commit v5 on v4

--- a/solution.py
+++ b/solution.py
@@ -349,7 +349,8 @@
         f = weight_halo[side, l] * (next_halo[j, l, side] - here)
         spread_halo[l, side] = coeff_halo[side, l, 1] * f
 
-    def finish(j, l, b):
+    def finish(j, l, order, at):
+        b = order[at]
         v, out = states[j], states[j + 1]
         side = side_of(b)
         f = follow[l, rows(b), :]
@@ -367,24 +368,25 @@
         came = before[j, l, rows(b), :]
         if side is not None:
             edges_from(FORE, j, l, side)
-            if j == 0 and l == 0 and side == 0:
+            if j == 0 and l == 0 and at == 0:
                 wait_if(has_prev, [centre_ahead()])
             came = came + edge_only(side, prev_centre[l, side] * prev_halo[j, l, side])
         out[l, rows(b), :] = SCALE * (out[l, rows(b), :] - weight[l, rows(b), :] * came)
         if j + 1 == STEPS:
+            keep(j, gram_block(j, l, rows(b), kept(j)))
             return
-        start_if(has_prev, [state_block(j + 1, l, b)])
         if side is not None:
             for n, row in enumerate(OUTER[side]):
                 edge[j + 1, l, side, n] = out[l, row : row + 1, :]
             send_edges(j + 1, l, side)
-        if b > 0:
-            propagate(j + 1, l, b - 1)
-        if b == BLOCKS - 1:
+        start_if(has_prev, [state_block(j + 1, l, b)])
+        if at > 0:
+            propagate(j + 1, l, order[at - 1])
+        if at == BLOCKS - 1:
             propagate(j + 1, l, b)
 
-    def complete(j, l):
-        for b in range(BLOCKS):
+    def complete(j, l, order):
+        for at, b in enumerate(order):
             side = side_of(b)
             if side is not None:
                 outside(j, l, side)
@@ -395,39 +397,50 @@
             f = next_weight[l, rows(b), :] * (next_state[j, l, rows(b), :] - sent_image)
             follow[l, rows(b), :] = f
             spread[l, rows(b), :] = coeff[1, l, rows(b), :] * f
-            if b > 0:
-                finish(j, l, b - 1)
-        finish(j, l, BLOCKS - 1)
-
-    def gram(group, l):
-        indices = range(3 * group, 3 * group + 3)
-        zero = jnp.zeros((8, 128), F32)
-
-        def step(b, acc):
-            acc = list(acc)
-            at = pl.ds(pl.multiple_of(b * 8, 8), 8)
-            for c in range(NX // 128):
-                parts = {}
-                for index in indices:
-                    for s in PAIRS[index]:
-                        if s not in parts:
-                            x = states[s][l, at, c * 128 : (c + 1) * 128]
-                            parts[s] = (x, split(x))
-                for n, index in enumerate(indices):
-                    i, k = PAIRS[index]
-                    p, e = two_prod_split(parts[i][0], parts[k][0], parts[i][1], parts[k][1])
-                    s, f = two_sum(acc[2 * n], p)
-                    acc[2 * n], acc[2 * n + 1] = s, acc[2 * n + 1] + (e + f)
-            return tuple(acc)
-
-        acc = lax.fori_loop(0, BLOCKS, step, (zero,) * 6)
-        for n, index in enumerate(indices):
-            part = (acc[2 * n], acc[2 * n + 1])
-            if l == 0:
-                gram_high[index], gram_low[index] = part
-                continue
-            part = over_rows(plus(part, (gram_high[index], gram_low[index])))
-            gram_line[index : index + 1, :], gram_line[16 + index : 17 + index, :] = part
+            if at > 0:
+                finish(j, l, order, at - 1)
+        finish(j, l, order, BLOCKS - 1)
+
+    def by_parity(body):
+        pl.when(tile % 2 == 0)(lambda: body(tuple(range(BLOCKS))))
+        pl.when(tile % 2 == 1)(lambda: body(tuple(reversed(range(BLOCKS)))))
+
+    def gram_block(group, l, at, acc):
+        acc = list(acc)
+        for c in range(NX // 128):
+            parts = {}
+            for n in range(3):
+                i, k = PAIRS[3 * group + n]
+                for s in (i, k):
+                    if s not in parts:
+                        x = states[s][l, at, c * 128 : (c + 1) * 128]
+                        parts[s] = (x, split(x))
+                p, e = two_prod_split(parts[i][0], parts[k][0], parts[i][1], parts[k][1])
+                s, f = two_sum(acc[2 * n], p)
+                acc[2 * n], acc[2 * n + 1] = s, acc[2 * n + 1] + (e + f)
+        return tuple(acc)
+
+    def keep(group, acc):
+        for n in range(3):
+            gram_high[3 * group + n], gram_low[3 * group + n] = acc[2 * n], acc[2 * n + 1]
+
+    def kept(group):
+        return tuple(ref[3 * group + n] for n in range(3) for ref in (gram_high, gram_low))
+
+    def gram_lines(group):
+        acc = kept(group)
+        for n in range(3):
+            index = 3 * group + n
+            line = over_rows((acc[2 * n], acc[2 * n + 1]))
+            gram_line[index : index + 1, :], gram_line[16 + index : 17 + index, :] = line
+
+    def gram(group):
+        def step(n, acc):
+            at = pl.ds(pl.multiple_of((n % BLOCKS) * 8, 8), 8)
+            return gram_block(group, n // BLOCKS, at, acc)
+
+        keep(group, lax.fori_loop(0, LEV * BLOCKS, step, (jnp.zeros((8, 128), F32),) * 6))
+        gram_lines(group)
 
     def over_rows(total):
         for shift in (4, 2, 1):
@@ -459,12 +472,18 @@
         for by in range(LEV):
             send_edges(0, by, side, diagonal=False)
         pl.when(beside[side])(lambda side=side: signal(known_sem.at[2, 0], towards(side, 0)))
-    blocks = [copy(l, b) for l in range(LEV) for b in range(BLOCKS) for copy in (first_block, weight_block)]
-    start_if(has_prev, blocks[:EARLY])
+    def bulk(order):
+        return [copy(l, b) for l in range(LEV) for b in order for copy in (first_block, weight_block)]
+
+    by_parity(lambda order: start_if(has_prev, bulk(order)[:EARLY]))
     loads[2].wait()
-    for l in range(LEV):
-        for b in range(BLOCKS):
-            propagate(0, l, b)
+
+    @by_parity
+    def _(order):
+        for l in range(LEV):
+            for b in order:
+                propagate(0, l, b)
+
     for at, move in enumerate((along_y, along_z)):
         for by in (1, -1):
             signal(known_sem.at[at, 0], move(by))
@@ -473,7 +492,7 @@
         start_if(and_(beside[side], has_prev), [weight_side(side)])
         for l in range(LEV):
             send_edges(0, l, side, straight=False)
-    start_if(has_prev, blocks[EARLY:])
+    by_parity(lambda order: start_if(has_prev, bulk(order)[EARLY:]))
     for side in range(2):
         row = OUTER[side][0]
         for l in range(LEV):
@@ -483,7 +502,7 @@
     for side in range(2):
         start_if(beside[side], [coeff_side(side)])
     start_if(has_next, [centre_ahead()])
-    start_if(has_next, [image_block(0, 1, b) for b in range(BLOCKS)])
+    by_parity(lambda order: start_if(has_next, [image_block(0, 1, b) for b in order]))
     for side in range(2):
 
         @pl.when(jnp.logical_not(beside[side]))
@@ -503,17 +522,17 @@
         for by in (2, -2):
             signal(known_sem.at[at, 1], move(by))
     for j in range(STEPS):
+        if j + 1 == STEPS:
+            keep(j, (jnp.zeros((8, 128), F32),) * 6)
         for l in range(LEV):
-            complete(j, l)
-            if j + 1 == STEPS:
-                gram(2, l)
+            by_parity(lambda order, j=j, l=l: complete(j, l, order))
         if j + 1 < STEPS:
             for at, move in enumerate((along_y, along_z)):
                 pl.semaphore_wait(known_sem.at[at, j + 1], 2)
                 for by in (1, -1) if j == 0 else ():
                     signal(known_sem.at[at, 2], move(by))
-            for l in range(LEV):
-                gram(j, l)
+            gram(j)
+    gram_lines(STEPS - 1)
 
     turned = jnp.swapaxes(gram_line[...], 0, 1)
     pieces = [turned[8 * i : 8 * i + 8, :] for i in range(16)]

time: 43.7 us -> 42.2 us (0.966)
  Pallas kernels: 42.9 us -> 41.5 us
    pallas_call x1, Pallas kernels: 42.1 us -> 40.6 us  [on_device(): pl.pallas_call(kernel, out_shape=(pltpu.VMEM((1, *shape), F32), pltpu.VME...]
where the time goes in v5:
time: 42.2 us; the launch traced here: 42.1 us
  Pallas kernels  41.5 us (98%)
  between operations  0.64 us (2%)
    pallas_call x1, Pallas kernels, on_device(): pl.pallas_call(kernel, out_shape=(pltpu.VMEM((1, *shape), F32), pltpu.VME...  40.6 us

profile of v5, /device:TPU:1, one launch (start us, length us, event | category | flops | bytes accessed | tf_op | source)
XLA Modules:
  0.0 42.1 jit_solution(17770029972886025614)
XLA Ops:
  0.6 40.6 %krylov.1 = (f32[1,2,32,1024]{3,2,1,0:T(8,128)S(1)}, f32[1,2,32,1024]{3,2,1,0:T(8,128)S(1)}) custom-call(f32[2,32,1024]{2,1,0:T(8,128)} %bitcast.6, f32[2,32,1024]{2,1,0:T(8,128)} %bitcast.7, f32[4,2,32,1024]{3,2,1,0:T(8,128)} %bitcast.5, s32[1,32]{1,0:T(1,128)} %block_hbm.1, s32[32,128]{1,0:T(8,128)} %bitcast.8, f32[32,128]{1,0:T(8,128)} %bitcast.9), custom_call_target="tpu_custom_call" | custom-call | tf_op jit(solution)/shard_map/krylov/pallas_call | solution.py:679
  41.3 0.8 %store.1 = (f32[1,2,32,1024]{3,2,1,0:T(8,128)}, f32[1,2,32,1024]{3,2,1,0:T(8,128)}) custom-call(f32[1,2,32,1024]{3,2,1,0:T(8,128)S(1)} %get-tuple-element.4.solution_field, f32[1,2,32,1024]{3,2,1,0:T(8,128)S(1)} %get-tuple-element.5.residual), custom_call_target="tpu_custom_call" | custom-call | tf_op jit(solution)/shard_map/store/pallas_call | solution.py:696

commit v6 on v5

--- a/solution.py
+++ b/solution.py
@@ -24,6 +24,7 @@
 BACK_SIDE_ROWS = LEV * (STEPS + 1) * WIDE
 AHEAD_SIDE_ROWS = LEV * STEPS * WIDE
 EARLY = 6
+MIDDLE = (1, 2)
 OUTER = ((0, 1), (TY - 1, TY - 2))
 
 
@@ -127,6 +128,8 @@
     prev_centre,
     next_state,
     next_weight,
+    term,
+    next_term,
     image,
     before,
     spread_halo,
@@ -138,6 +141,8 @@
     row_send,
     row_recv,
     plane_recv,
+    far_recv,
+    final_line,
     local_sem,
     send_sem,
     recv_sem,
@@ -283,6 +288,15 @@
             weight.at[l, at], next_weight.at[l, at], send_sem.at[2], once_sem.at[5 + BLOCKS * l + b], prev_id
         )
 
+    def term_block(b):
+        n = MIDDLE.index(b)
+        return remote(
+            term.at[n], next_term.at[n], send_sem.at[2], once_sem.at[5 + BLOCKS * LEV + n], prev_id
+        )
+
+    def from_next(j, l, b):
+        return j == 0 and l == LEV - 1 and b in MIDDLE
+
     def coeff_side(side):
         return remote(
             coeff_edge.at[side], coeff_halo.at[1 - side], send_sem.at[side], once_sem.at[1 - side], towards(side, 0)
@@ -326,7 +340,7 @@
             + coeff[2, l, rows(b), :] * pltpu.roll(here, NX - 1, 1)
             + coeff[3, l, rows(b), :] * pltpu.roll(here, 1, 1)
         )
-        if j > 0 or l == 0:
+        if j > 0 or l == 0 or from_next(j, l, b):
             start_if(has_next, [image_block(j, l, b)])
 
     def side_of(b):
@@ -364,7 +378,8 @@
         )
         here = v[l, rows(b), :]
         out[l, rows(b), :] = weight[l, rows(b), :] * here - back_image + diag[l, rows(b), :] * here
-        wait_if(has_prev, [image_block(j, l, b)])
+        if not from_next(j, l, b):
+            wait_if(has_prev, [image_block(j, l, b)])
         came = before[j, l, rows(b), :]
         if side is not None:
             edges_from(FORE, j, l, side)
@@ -390,11 +405,16 @@
             side = side_of(b)
             if side is not None:
                 outside(j, l, side)
-            wait_if(has_next, [state_block(j, l, b), *([weight_block(l, b)] if j == 0 else [])])
-            sent_image = image[j, l, rows(b), :]
-            if side is not None:
-                sent_image = sent_image + edge_only(side, coeff[1, l, rows(b), :] * halo[j, l, side, 0])
-            f = next_weight[l, rows(b), :] * (next_state[j, l, rows(b), :] - sent_image)
+            if from_next(j, l, b):
+                wait_if(has_next, [term_block(b)])
+                f = next_term[MIDDLE.index(b)]
+            else:
+                first = j == (1 if from_next(0, l, b) else 0)
+                wait_if(has_next, [state_block(j, l, b), *([weight_block(l, b)] if first else [])])
+                sent_image = image[j, l, rows(b), :]
+                if side is not None:
+                    sent_image = sent_image + edge_only(side, coeff[1, l, rows(b), :] * halo[j, l, side, 0])
+                f = next_weight[l, rows(b), :] * (next_state[j, l, rows(b), :] - sent_image)
             follow[l, rows(b), :] = f
             spread[l, rows(b), :] = coeff[1, l, rows(b), :] * f
             if at > 0:
@@ -473,20 +493,27 @@
             send_edges(0, by, side, diagonal=False)
         pl.when(beside[side])(lambda side=side: signal(known_sem.at[2, 0], towards(side, 0)))
     def bulk(order):
-        return [copy(l, b) for l in range(LEV) for b in order for copy in (first_block, weight_block)]
+        places = [(l, b) for l in range(LEV) for b in order if not from_next(0, l, b)]
+        return [copy(*place) for place in places for copy in (first_block, weight_block)]
 
     by_parity(lambda order: start_if(has_prev, bulk(order)[:EARLY]))
     loads[2].wait()
 
     @by_parity
     def _(order):
-        for l in range(LEV):
-            for b in order:
-                propagate(0, l, b)
-
-    for at, move in enumerate((along_y, along_z)):
-        for by in (1, -1):
-            signal(known_sem.at[at, 0], move(by))
+        places = [(l, b) for l in range(LEV) for b in order]
+        for place in sorted(places, key=lambda place: not from_next(0, *place)):
+            propagate(0, *place)
+
+    def pass_on(number):
+        if number > 0:
+            pl.semaphore_wait(known_sem.at[(number - 1) // 3, (number - 1) % 3], 2)
+        if number < 6:
+            move, by = (along_y, along_z)[number // 3], (1, 2, 1)[number % 3]
+            for peer in (move(by), move(-by)):
+                signal(known_sem.at[number // 3, number % 3], peer)
+
+    pass_on(0)
     pl.semaphore_wait(known_sem.at[2, 0], jnp.where(has_north, 1, 0) + jnp.where(has_south, 1, 0))
     for side in range(2):
         start_if(and_(beside[side], has_prev), [weight_side(side)])
@@ -502,7 +529,7 @@
     for side in range(2):
         start_if(beside[side], [coeff_side(side)])
     start_if(has_next, [centre_ahead()])
-    by_parity(lambda order: start_if(has_next, [image_block(0, 1, b) for b in order]))
+    by_parity(lambda order: start_if(has_next, [image_block(0, 1, b) for b in order if b not in MIDDLE]))
     for side in range(2):
 
         @pl.when(jnp.logical_not(beside[side]))
@@ -513,24 +540,29 @@
                     zeros(halo.at[j, l, side], next_halo.at[j, l, side], prev_halo.at[j, l, side])
 
     pl.when(jnp.logical_not(has_prev))(lambda: zeros(before, prev_halo, prev_centre))
-    pl.when(jnp.logical_not(has_next))(lambda: zeros(next_state, next_weight, next_halo, weight_halo))
+    pl.when(jnp.logical_not(has_next))(lambda: zeros(next_state, next_weight, next_term, next_halo, weight_halo))
     for load in loads[3:]:
         load.wait()
     observed_weights()
-    for at, move in enumerate((along_y, along_z)):
-        pl.semaphore_wait(known_sem.at[at, 0], 2)
-        for by in (2, -2):
-            signal(known_sem.at[at, 1], move(by))
+    pass_on(1)
+    @by_parity
+    def _(order):
+        l = LEV - 1
+        inner = [b for b in order if b in MIDDLE]
+        for b in inner:
+            wait_if(has_prev, [image_block(0, l, b)])
+            term[MIDDLE.index(b)] = weight[l, rows(b), :] * (v0[l, rows(b), :] - before[0, l, rows(b), :])
+            start_if(has_prev, [term_block(b)])
+        start_if(has_prev, [weight_block(l, b) for b in inner])
+
     for j in range(STEPS):
         if j + 1 == STEPS:
             keep(j, (jnp.zeros((8, 128), F32),) * 6)
         for l in range(LEV):
             by_parity(lambda order, j=j, l=l: complete(j, l, order))
+            if j * LEV + l < 5:
+                pass_on(j * LEV + l + 2)
         if j + 1 < STEPS:
-            for at, move in enumerate((along_y, along_z)):
-                pl.semaphore_wait(known_sem.at[at, j + 1], 2)
-                for by in (1, -1) if j == 0 else ():
-                    signal(known_sem.at[at, 2], move(by))
             gram(j)
     gram_lines(STEPS - 1)
 
@@ -551,46 +583,66 @@
         whole = ballast.at[pl.ds(0, count)]
         pltpu.make_async_copy(whole, whole, rrecv_sem.at[stage]).wait()
 
-    def to_plane(by, x_by):
-        where = (along_y(by)[0] - core + 1, (tile + x_by) % NT)
+    def to_plane(y, x):
+        where = (win - core + 1 + 2 * (y - chip_y), x)
         return remote(
             row_send.at[0], plane_recv.at[pl.ds(slot_a, 1)], send_sem.at[8], rrecv_sem.at[0], where
         )
 
-    def to_z(by, other_core):
-        return remote(
-            row_send.at[1], row_recv.at[chip_z], send_sem.at[9], rrecv_sem.at[1], along_z(by, other_core)
+    def to_z(z, other_core):
+        peer = (win + 16 * (z - chip_z) - other_core, tile)
+        return remote(row_send.at[1], row_recv.at[chip_z], send_sem.at[9], rrecv_sem.at[1], peer)
+
+    def to_first():
+        return remote(
+            row_send.at[0],
+            far_recv.at[pl.ds(jnp.maximum(win * NT + tile - PLANE, 0), 1)],
+            send_sem.at[8],
+            rrecv_sem.at[2],
+            (1, 0),
         )
 
     is_second = core == 1
+    in_first_column = and_(is_second, chip_y == 0, tile == 0)
+    is_first = and_(in_first_column, chip_z == 0)
     row_send[0] = line
-    for by in (4, 3, 5, 2, 6, 1, 7, 0):
-        for other in (2, 1, 3, 0):
-            copy = to_plane(by, other)
-            if by == 0 and other == 0:
-                pl.when(core == 0)(copy.start)
-            else:
-                copy.start()
+    start_if(chip_z > 0, [to_first()])
+    for y in range(NYC):
+        for x in range(NT):
+            start_if(jnp.logical_or(core == 0, chip_y * NT + tile != y * NT + x), [to_plane(y, x)])
 
     @pl.when(is_second)
     def _():
         plane_recv[pl.ds(slot_a, 1), :] = line
         arrived(0, PLANE - 1)
-        mine = packed(over_slots([plane_recv[8 * i : 8 * i + 8, :] for i in range(PLANE // 8)]))
+        plane = over_slots([plane_recv[8 * i : 8 * i + 8, :] for i in range(PLANE // 8)])
+        mine = packed(plane)
         row_send[1] = mine
         row_recv[chip_z] = mine
-        for by in (4, 3, 5, 2, 6, 1, 7):
-            to_z(by, True).start()
-            to_z(by, False).start()
-        to_z(0, True).start()
-        arrived(1, NZ - 1)
+        for z in range(NZ):
+            start_if(and_(chip_z != z, jnp.logical_not(in_first_column) if z == 0 else chip_z != z), [to_z(z, 0)])
+            to_z(z, 1).start()
+
+        @pl.when(jnp.logical_not(is_first))
+        def _():
+            arrived(1, NZ - 1)
+
+        @pl.when(is_first)
+        def _():
+            arrived(2, NWIN * NT - PLANE)
+            far = over_slots([far_recv[8 * i : 8 * i + 8, :] for i in range((NWIN * NT - PLANE) // 8)])
+            final_line[...] = packed(quick_sum(*plus(plane, far)))
 
     @pl.when(jnp.logical_not(is_second))
     def _():
         arrived(1, NZ)
 
-    total = tree2([(x, pltpu.roll(x, 128 - 16, 1)) for x in [row_recv[i] for i in range(NZ)]])
-    line = packed(quick_sum(*total))
+    @pl.when(jnp.logical_not(is_first))
+    def _():
+        total = tree2([(x, pltpu.roll(x, 128 - 16, 1)) for x in [row_recv[i] for i in range(NZ)]])
+        final_line[...] = packed(quick_sum(*total))
+
+    line = final_line[...]
 
     def value(i, j):
         at = PAIRS.index((min(i, j), max(i, j)))
@@ -602,10 +654,12 @@
             factor = div2(a[i][pivot], a[pivot][pivot])
             for n in range(pivot + 1, 4):
                 a[i][n] = sub2(a[i][n], mul2(factor, a[pivot][n]))
-    c2 = div2(a[2][3], a[2][2])
-    c1 = div2(sub2(a[1][3], mul2(a[1][2], c2)), a[1][1])
-    c0 = div2(sub2(sub2(a[0][3], mul2(a[0][1], c1)), mul2(a[0][2], c2)), a[0][0])
-    combo = [jnp.concatenate([c[0]] * (NX // 128), axis=1) for c in (c0, c1, c2)]
+    zero = jnp.zeros((8, 128), F32)
+    c2 = a[2][3][0] / a[2][2][0]
+    c1 = sub2(a[1][3], mul2(a[1][2], (c2, zero)))[0] / a[1][1][0]
+    left = sub2(a[0][3], mul2(a[0][1], (c1, zero)))
+    c0 = sub2(left, mul2(a[0][2], (c2, zero)))[0] / a[0][0][0]
+    combo = [jnp.concatenate([c] * (NX // 128), axis=1) for c in (c0, c1, c2)]
     for l in range(LEV):
         for b in range(BLOCKS):
             at = (l, rows(b), slice(None))
@@ -625,9 +679,13 @@
         sent(and_(beside[side], has_next), AHEAD_SIDE_ROWS, send_sem.at[6 + side])
     sent(has_prev, BACK_ROWS, send_sem.at[2])
     sent(has_next, AHEAD_ROWS, send_sem.at[3])
-    sent(is_second, PLANE // 2 - 1, send_sem.at[8])
-    sent(jnp.logical_not(is_second), PLANE // 2, send_sem.at[8])
-    sent(is_second, 2 * NZ - 1, send_sem.at[9])
+    more = jnp.where(chip_z > 0, 1, 0)
+    sent_lines = PLANE // 2 - core + more
+    for count in (PLANE // 2 - 1, PLANE // 2, PLANE // 2 + 1):
+        sent(sent_lines == count, count, send_sem.at[8])
+    skips_first = and_(in_first_column, chip_z > 0)
+    sent(and_(is_second, jnp.logical_not(skips_first)), 2 * NZ - 1, send_sem.at[9])
+    sent(skips_first, 2 * NZ - 2, send_sem.at[9])
 
 
 def on_device(right_side, error_weight, coeffs, obs_block, obs_pos, obs_weight):
@@ -657,6 +715,8 @@
         vmem((LEV, 2, 1, NX), F32),
         vmem((STEPS, *shape), F32),
         vmem(shape, F32),
+        vmem((2, 8, NX), F32),
+        vmem((2, 8, NX), F32),
         vmem((STEPS, *shape), F32),
         vmem((STEPS, *shape), F32),
         vmem((LEV, 2, 1, NX), F32),
@@ -668,11 +728,13 @@
         vmem((2, 1, 128), F32),
         vmem((NZ, 1, 128), F32),
         vmem((PLANE, 128), F32),
+        vmem((NWIN * NT - PLANE, 128), F32),
+        vmem((1, 128), F32),
         pltpu.SemaphoreType.DMA((6,)),
         pltpu.SemaphoreType.DMA((10,)),
         pltpu.SemaphoreType.DMA((2, LEV, MESSAGES)),
-        pltpu.SemaphoreType.DMA((5 + LEV * BLOCKS,)),
-        pltpu.SemaphoreType.DMA((2,)),
+        pltpu.SemaphoreType.DMA((5 + LEV * BLOCKS + 2,)),
+        pltpu.SemaphoreType.DMA((3,)),
         pltpu.SemaphoreType.REGULAR((3, 3)),
         vmem((BACK_ROWS, 1, 128), F32),
     ]

time: 42.2 us -> 40.6 us (0.962)
  Pallas kernels: 41.5 us -> 39.9 us
    pallas_call x1, Pallas kernels: 40.6 us -> 39.1 us  [on_device(): pl.pallas_call(kernel, out_shape=(pltpu.VMEM((1, *shape), F32), pltpu.VME...]
where the time goes in v6:
time: 40.6 us; the launch traced here: 40.5 us
  Pallas kernels  39.9 us (98%)
  between operations  0.64 us (2%)
    pallas_call x1, Pallas kernels, on_device(): pl.pallas_call(kernel, out_shape=(pltpu.VMEM((1, *shape), F32), pltpu.VME...  39.1 us

profile of v6, /device:TPU:1, one launch (start us, length us, event | category | flops | bytes accessed | tf_op | source)
XLA Modules:
  0.0 40.5 jit_solution(10922290876363887310)
XLA Ops:
  0.6 39.1 %krylov.1 = (f32[1,2,32,1024]{3,2,1,0:T(8,128)S(1)}, f32[1,2,32,1024]{3,2,1,0:T(8,128)S(1)}) custom-call(f32[2,32,1024]{2,1,0:T(8,128)} %bitcast.6, f32[2,32,1024]{2,1,0:T(8,128)} %bitcast.7, f32[4,2,32,1024]{3,2,1,0:T(8,128)} %bitcast.5, s32[1,32]{1,0:T(1,128)} %block_hbm.1, s32[32,128]{1,0:T(8,128)} %bitcast.8, f32[32,128]{1,0:T(8,128)} %bitcast.9), custom_call_target="tpu_custom_call" | custom-call | tf_op jit(solution)/shard_map/krylov/pallas_call | solution.py:741
  39.7 0.8 %store.1 = (f32[1,2,32,1024]{3,2,1,0:T(8,128)}, f32[1,2,32,1024]{3,2,1,0:T(8,128)}) custom-call(f32[1,2,32,1024]{3,2,1,0:T(8,128)S(1)} %get-tuple-element.4.solution_field, f32[1,2,32,1024]{3,2,1,0:T(8,128)S(1)} %get-tuple-element.5.residual), custom_call_target="tpu_custom_call" | custom-call | tf_op jit(solution)/shard_map/store/pallas_call | solution.py:758

commit v7 on v6

--- a/solution.py
+++ b/solution.py
@@ -189,8 +189,8 @@
     near = [
         (win - core + ((group + i) % 8) // NT, (group + i) % NT) for i in range(1, NCORE * NT)
     ]
-    near += [along_y(1), along_y(-1)]
-    near += [along_z(by, other) for by in (1, -1) for other in (False, True)]
+    near = [along_y(1), along_y(-1)] + near
+    near = [along_z(by, other) for by in (1, -1) for other in (False, True)] + near
 
     def signal(semaphore, peer):
         pl.semaphore_signal(semaphore, inc=1, device_id=peer, device_id_type=MESH)
@@ -219,6 +219,12 @@
 
     pl.semaphore_wait(barrier, len(near) + jnp.where(has_prev, 1, 0) + jnp.where(has_next, 1, 0))
 
+    def whole_if(condition, count, semaphore):
+        @pl.when(condition)
+        def _():
+            whole = ballast.at[pl.ds(0, count)]
+            pltpu.make_async_copy(whole, whole, semaphore).wait()
+
     def remote(src, dst, send, recv, peer):
         return pltpu.make_async_remote_copy(
             src_ref=src, dst_ref=dst, send_sem=send, recv_sem=recv, device_id=peer, device_id_type=MESH
@@ -284,14 +290,15 @@
 
     def weight_block(l, b):
         at = pl.ds(8 * b, 8)
-        return remote(
-            weight.at[l, at], next_weight.at[l, at], send_sem.at[2], once_sem.at[5 + BLOCKS * l + b], prev_id
+        late = int(from_next(0, l, b))
+        return remote(
+            weight.at[l, at], next_weight.at[l, at], send_sem.at[2], recv_sem.at[late, l, STATE + b], prev_id
         )
 
     def term_block(b):
         n = MIDDLE.index(b)
         return remote(
-            term.at[n], next_term.at[n], send_sem.at[2], once_sem.at[5 + BLOCKS * LEV + n], prev_id
+            term.at[n], next_term.at[n], send_sem.at[2], recv_sem.at[0, LEV - 1, STATE + b], prev_id
         )
 
     def from_next(j, l, b):
@@ -299,7 +306,7 @@
 
     def coeff_side(side):
         return remote(
-            coeff_edge.at[side], coeff_halo.at[1 - side], send_sem.at[side], once_sem.at[1 - side], towards(side, 0)
+            coeff_edge.at[side], coeff_halo.at[1 - side], send_sem.at[side], recv_sem.at[0, 0, HALO + 1 - side], towards(side, 0)
         )
 
     def weight_side(side):
@@ -307,12 +314,12 @@
             weight_edge.at[side],
             weight_halo.at[1 - side],
             send_sem.at[4 + side],
-            once_sem.at[3 - side],
+            recv_sem.at[0, 0, BACK + 1 - side],
             towards(side, -1),
         )
 
     def centre_ahead():
-        return remote(centre_edge, prev_centre, send_sem.at[3], once_sem.at[4], next_id)
+        return remote(centre_edge, prev_centre, send_sem.at[3], once_sem.at[0], next_id)
 
     row_id = lax.broadcasted_iota(jnp.int32, (8, NX), 0)
     first_row, last_row = row_id == 0, row_id == 7
@@ -347,10 +354,11 @@
         return {0: 0, BLOCKS - 1: 1}.get(b)
 
     def outside(j, l, side):
-        edges_from(HALO, j, l, side)
-        if j == 0 and l == 0:
-            wait_if(beside[side], [coeff_side(1 - side)])
-            wait_if(and_(beside[side], has_next), [weight_side(1 - side)])
+        first = j == 0 and l == 0
+        if first:
+            whole_if(beside[side], (2 + LEV * 4) * WIDE, recv_sem.at[0, 0, HALO + side])
+        else:
+            edges_from(HALO, j, l, side)
         near_row, far_row = halo[j, l, side, 0], halo[j, l, side, 1]
         row = OUTER[side][0]
         here = (
@@ -359,7 +367,10 @@
             + coeff_halo[side, l, 2] * pltpu.roll(near_row, NX - 1, 1)
             + coeff_halo[side, l, 3] * pltpu.roll(near_row, 1, 1)
         )
-        edges_from(BACK, j, l, side)
+        if first:
+            whole_if(and_(beside[side], has_next), (1 + LEV) * WIDE, recv_sem.at[0, 0, BACK + side])
+        else:
+            edges_from(BACK, j, l, side)
         f = weight_halo[side, l] * (next_halo[j, l, side] - here)
         spread_halo[l, side] = coeff_halo[side, l, 1] * f
 
@@ -410,7 +421,10 @@
                 f = next_term[MIDDLE.index(b)]
             else:
                 first = j == (1 if from_next(0, l, b) else 0)
-                wait_if(has_next, [state_block(j, l, b), *([weight_block(l, b)] if first else [])])
+                if first:
+                    whole_if(has_next, 2 * 8 * WIDE, recv_sem.at[j, l, STATE + b])
+                else:
+                    wait_if(has_next, [state_block(j, l, b)])
                 sent_image = image[j, l, rows(b), :]
                 if side is not None:
                     sent_image = sent_image + edge_only(side, coeff[1, l, rows(b), :] * halo[j, l, side, 0])
@@ -491,7 +505,7 @@
     for side in range(2):
         for by in range(LEV):
             send_edges(0, by, side, diagonal=False)
-        pl.when(beside[side])(lambda side=side: signal(known_sem.at[2, 0], towards(side, 0)))
+        pl.when(beside[side])(lambda side=side: signal(known_sem.at[6], towards(side, 0)))
     def bulk(order):
         places = [(l, b) for l in range(LEV) for b in order if not from_next(0, l, b)]
         return [copy(*place) for place in places for copy in (first_block, weight_block)]
@@ -507,14 +521,14 @@
 
     def pass_on(number):
         if number > 0:
-            pl.semaphore_wait(known_sem.at[(number - 1) // 3, (number - 1) % 3], 2)
+            pl.semaphore_wait(known_sem.at[number - 1], 2)
         if number < 6:
             move, by = (along_y, along_z)[number // 3], (1, 2, 1)[number % 3]
             for peer in (move(by), move(-by)):
-                signal(known_sem.at[number // 3, number % 3], peer)
+                signal(known_sem.at[number], peer)
 
     pass_on(0)
-    pl.semaphore_wait(known_sem.at[2, 0], jnp.where(has_north, 1, 0) + jnp.where(has_south, 1, 0))
+    pl.semaphore_wait(known_sem.at[6], jnp.where(has_north, 1, 0) + jnp.where(has_south, 1, 0))
     for side in range(2):
         start_if(and_(beside[side], has_prev), [weight_side(side)])
         for l in range(LEV):
@@ -667,25 +681,19 @@
             solution_out[0, l, rows(b), :] = SCALE * (combo[0] * u0 + combo[1] * u1 + combo[2] * u2)
             residual_out[0, l, rows(b), :] = u0 - combo[0] * u1 - combo[1] * u2 - combo[2] * u3
 
-    def sent(condition, count, semaphore):
-        @pl.when(condition)
-        def _():
-            whole = ballast.at[pl.ds(0, count)]
-            pltpu.make_async_copy(whole, whole, semaphore).wait()
-
     for side in range(2):
-        sent(beside[side], SIDE_ROWS, send_sem.at[side])
-        sent(and_(beside[side], has_prev), BACK_SIDE_ROWS, send_sem.at[4 + side])
-        sent(and_(beside[side], has_next), AHEAD_SIDE_ROWS, send_sem.at[6 + side])
-    sent(has_prev, BACK_ROWS, send_sem.at[2])
-    sent(has_next, AHEAD_ROWS, send_sem.at[3])
+        whole_if(beside[side], SIDE_ROWS, send_sem.at[side])
+        whole_if(and_(beside[side], has_prev), BACK_SIDE_ROWS, send_sem.at[4 + side])
+        whole_if(and_(beside[side], has_next), AHEAD_SIDE_ROWS, send_sem.at[6 + side])
+    whole_if(has_prev, BACK_ROWS, send_sem.at[2])
+    whole_if(has_next, AHEAD_ROWS, send_sem.at[3])
     more = jnp.where(chip_z > 0, 1, 0)
     sent_lines = PLANE // 2 - core + more
     for count in (PLANE // 2 - 1, PLANE // 2, PLANE // 2 + 1):
-        sent(sent_lines == count, count, send_sem.at[8])
+        whole_if(sent_lines == count, count, send_sem.at[8])
     skips_first = and_(in_first_column, chip_z > 0)
-    sent(and_(is_second, jnp.logical_not(skips_first)), 2 * NZ - 1, send_sem.at[9])
-    sent(skips_first, 2 * NZ - 2, send_sem.at[9])
+    whole_if(and_(is_second, jnp.logical_not(skips_first)), 2 * NZ - 1, send_sem.at[9])
+    whole_if(skips_first, 2 * NZ - 2, send_sem.at[9])
 
 
 def on_device(right_side, error_weight, coeffs, obs_block, obs_pos, obs_weight):
@@ -733,9 +741,9 @@
         pltpu.SemaphoreType.DMA((6,)),
         pltpu.SemaphoreType.DMA((10,)),
         pltpu.SemaphoreType.DMA((2, LEV, MESSAGES)),
-        pltpu.SemaphoreType.DMA((5 + LEV * BLOCKS + 2,)),
+        pltpu.SemaphoreType.DMA((1,)),
         pltpu.SemaphoreType.DMA((3,)),
-        pltpu.SemaphoreType.REGULAR((3, 3)),
+        pltpu.SemaphoreType.REGULAR((7,)),
         vmem((BACK_ROWS, 1, 128), F32),
     ]
     solution_field, residual = pl.pallas_call(
@@ -760,15 +768,16 @@
         out_shape=(whole, whole),
         in_specs=[pl.BlockSpec(memory_space=vmem)] * 2,
         out_specs=(pl.BlockSpec(memory_space=hbm),) * 2,
-        scratch_shapes=[pltpu.SemaphoreType.DMA((2,))],
+        scratch_shapes=[pltpu.SemaphoreType.DMA((2 * LEV,))],
         name="store",
     )(*(pltpu.with_memory_space_constraint(x, vmem) for x in (solution_field, residual)))
 
 
 def store(solution_field, residual, solution_out, residual_out, sem):
     copies = [
-        pltpu.make_async_copy(solution_field, solution_out, sem.at[0]),
-        pltpu.make_async_copy(residual, residual_out, sem.at[1]),
+        pltpu.make_async_copy(src.at[0, l], dst.at[0, l], sem.at[LEV * n + l])
+        for n, (src, dst) in enumerate(((solution_field, solution_out), (residual, residual_out)))
+        for l in range(LEV)
     ]
     for copy in copies:
         copy.start()

time: 40.6 us -> 40.5 us (level)
  no operation moved by 1% of the time
where the time goes in v7:
time: 40.5 us; the launch traced here: 40.4 us
  Pallas kernels  39.8 us (98%)
  between operations  0.64 us (2%)
    pallas_call x1, Pallas kernels, on_device(): pl.pallas_call(kernel, out_shape=(pltpu.VMEM((1, *shape), F32), pltpu.VME...  38.9 us
    pallas_call x1, Pallas kernels, on_device(): pl.pallas_call(store, out_shape=(whole, whole), in_specs=[pl.BlockSpec(me...  0.82 us

profile of v7, /device:TPU:1, one launch (start us, length us, event | category | flops | bytes accessed | tf_op | source)
XLA Modules:
  0.0 40.4 jit_solution(1205891884425553354)
XLA Ops:
  0.6 38.9 %krylov.1 = (f32[1,2,32,1024]{3,2,1,0:T(8,128)S(1)}, f32[1,2,32,1024]{3,2,1,0:T(8,128)S(1)}) custom-call(f32[2,32,1024]{2,1,0:T(8,128)} %bitcast.6, f32[2,32,1024]{2,1,0:T(8,128)} %bitcast.7, f32[4,2,32,1024]{3,2,1,0:T(8,128)} %bitcast.5, s32[1,32]{1,0:T(1,128)} %block_hbm.1, s32[32,128]{1,0:T(8,128)} %bitcast.8, f32[32,128]{1,0:T(8,128)} %bitcast.9), custom_call_target="tpu_custom_call" | custom-call | tf_op jit(solution)/shard_map/krylov/pallas_call | solution.py:749
  39.6 0.8 %store.1 = (f32[1,2,32,1024]{3,2,1,0:T(8,128)}, f32[1,2,32,1024]{3,2,1,0:T(8,128)}) custom-call(f32[1,2,32,1024]{3,2,1,0:T(8,128)S(1)} %get-tuple-element.4.solution_field, f32[1,2,32,1024]{3,2,1,0:T(8,128)S(1)} %get-tuple-element.5.residual), custom_call_target="tpu_custom_call" | custom-call | tf_op jit(solution)/shard_map/store/pallas_call | solution.py:766

commit v8 on v7

--- a/solution.py
+++ b/solution.py
@@ -263,11 +263,11 @@
         )
 
     def send_edges(j, l, side, diagonal=True, straight=True):
-        if straight:
-            start_if(beside[side], [to_side(HALO, j, l, side)])
         if diagonal:
             start_if(and_(beside[side], has_prev), [to_side(BACK, j, l, side)])
             start_if(and_(beside[side], has_next), [to_side(FORE, j, l, side)])
+        if straight:
+            start_if(beside[side], [to_side(HALO, j, l, side)])
 
     def edges_from(kind, j, l, side):
         extra = {HALO: (), BACK: (has_next,), FORE: (has_prev,)}[kind]

time: 40.5 us -> 40.5 us (level)
  no operation moved by 1% of the time
where the time goes in v8:
time: 40.5 us; the launch traced here: 40.4 us
  Pallas kernels  39.8 us (98%)
  between operations  0.64 us (2%)
    pallas_call x1, Pallas kernels, on_device(): pl.pallas_call(kernel, out_shape=(pltpu.VMEM((1, *shape), F32), pltpu.VME...  38.9 us
    pallas_call x1, Pallas kernels, on_device(): pl.pallas_call(store, out_shape=(whole, whole), in_specs=[pl.BlockSpec(me...  0.82 us

profile of v8, /device:TPU:1, one launch (start us, length us, event | category | flops | bytes accessed | tf_op | source)
XLA Modules:
  0.0 40.4 jit_solution(355622447139921021)
XLA Ops:
  0.6 38.9 %krylov.1 = (f32[1,2,32,1024]{3,2,1,0:T(8,128)S(1)}, f32[1,2,32,1024]{3,2,1,0:T(8,128)S(1)}) custom-call(f32[2,32,1024]{2,1,0:T(8,128)} %bitcast.6, f32[2,32,1024]{2,1,0:T(8,128)} %bitcast.7, f32[4,2,32,1024]{3,2,1,0:T(8,128)} %bitcast.5, s32[1,32]{1,0:T(1,128)} %block_hbm.1, s32[32,128]{1,0:T(8,128)} %bitcast.8, f32[32,128]{1,0:T(8,128)} %bitcast.9), custom_call_target="tpu_custom_call" | custom-call | tf_op jit(solution)/shard_map/krylov/pallas_call | solution.py:749
  39.6 0.8 %store.1 = (f32[1,2,32,1024]{3,2,1,0:T(8,128)}, f32[1,2,32,1024]{3,2,1,0:T(8,128)}) custom-call(f32[1,2,32,1024]{3,2,1,0:T(8,128)S(1)} %get-tuple-element.4.solution_field, f32[1,2,32,1024]{3,2,1,0:T(8,128)S(1)} %get-tuple-element.5.residual), custom_call_target="tpu_custom_call" | custom-call | tf_op jit(solution)/shard_map/store/pallas_call | solution.py:766
